TPU v7x, 32 devices: a 4x4x1 block of a 4x4x8 slice. The times are simulated.
32 devices in a mesh: rep: 1 (over z), heads: 4 (over y), pool: 8 (over x, core).
Axes of the slice: x: 4, y: 4, z: 1, core: 2. Of those that a mesh axis runs over, the one named last changes fastest.
The devices are a block of a 4x4x8 slice.
Arguments:
- kv_pool: bfloat16 [1, 128, 2, 128, 32, 128], P(None, ('rep', 'pool'), None, None, 'heads')
- page_idx: int32 [8, 8, 1], P('rep', 'pool')
- x_tokens: bfloat16 [8, 512, 4096], P(('rep', 'pool'))
- gain_attn: bfloat16 [1, 4096], replicated
- w_q: bfloat16 [1, 4096, 4096], P(None, None, 'heads')
- w_k: bfloat16 [1, 4096, 4096], P(None, None, 'heads')
- w_v: bfloat16 [1, 4096, 4096], P(None, None, 'heads')
- w_o: bfloat16 [1, 4096, 4096], P(None, 'heads')
- gain_mlp: bfloat16 [1, 4096], replicated
- w_gate: bfloat16 [1, 4096, 11008], P(None, None, 'heads')
- w_up: bfloat16 [1, 4096, 11008], P(None, None, 'heads')
- w_down: bfloat16 [1, 11008, 4096], P(None, 'heads')
Outputs:
- output: bfloat16 [8, 512, 4096], P(('rep', 'pool'))
All inputs are finite; a program needn't handle non-finite values.
Results may differ from a plain program's by a relative error of at most 0.0130825.
Values are sent between devices in bfloat16 or wider.
A program may use at most 768 MiB of HBM per device.

v0:
```python
import jax
import jax.numpy as jnp
from jax import lax
from jax.sharding import PartitionSpec as P


def rms_norm(hidden, gain_vec):
    hid_f32 = hidden.astype(jnp.float32)
    inv_rms = lax.rsqrt(jnp.mean(hid_f32 * hid_f32, axis=-1, keepdims=True) + 1e-5)
    return (hid_f32 * inv_rms * gain_vec.astype(jnp.float32)).astype(jnp.bfloat16)


def rope_tables(prefix, tokens, head_dim):
    positions = (prefix + jnp.arange(tokens)).astype(jnp.float32)
    inv_freq = 10000.0 ** (-2.0 * jnp.arange(head_dim // 2).astype(jnp.float32) / head_dim)
    angles = positions[:, None] * inv_freq[None, :]
    return jnp.cos(angles)[:, None, :], jnp.sin(angles)[:, None, :]


def apply_rope(projected, cos_tab, sin_tab):
    half_dim = projected.shape[-1] // 2
    first_half = projected[..., :half_dim]
    second_half = projected[..., half_dim:]
    return jnp.concatenate([first_half * cos_tab - second_half * sin_tab, second_half * cos_tab + first_half * sin_tab], axis=-1)


def attend(queries, keys_pre, vals_pre, k_new, v_new, causal):
    score_scale = queries.shape[-1] ** -0.5
    s_pre = jnp.einsum('tgrd,ngd->grtn', queries, keys_pre, preferred_element_type=jnp.float32) * score_scale
    s_new = jnp.einsum('tgrd,ngd->grtn', queries, k_new, preferred_element_type=jnp.float32) * score_scale
    s_new = jnp.where(causal, s_new, -jnp.inf)
    row_max = jnp.maximum(jnp.max(s_pre, axis=-1, keepdims=True), jnp.max(s_new, axis=-1, keepdims=True))
    e_pre = jnp.exp(s_pre - row_max)
    e_new = jnp.exp(s_new - row_max)
    inv_den = 1.0 / (jnp.sum(e_pre, axis=-1, keepdims=True) + jnp.sum(e_new, axis=-1, keepdims=True))
    p_pre = (e_pre * inv_den).astype(jnp.bfloat16)
    p_new = (e_new * inv_den).astype(jnp.bfloat16)
    attn_sum = jnp.einsum('grtn,ngd->tgrd', p_pre, vals_pre, preferred_element_type=jnp.float32)
    attn_sum = attn_sum + jnp.einsum('grtn,ngd->tgrd', p_new, v_new, preferred_element_type=jnp.float32)
    return attn_sum.astype(jnp.bfloat16)


def solution(mesh):
    owners = mesh.shape['pool']

    def local_fn(kv_pool, page_idx, x_tokens, gain_attn, w_q, w_k, w_v, w_o, gain_mlp, w_gate, w_up, w_down):
        layers, _, _, page_len, kv_loc, head_dim = kv_pool.shape
        tokens = x_tokens.shape[1]
        req_pages = page_idx.shape[2]
        q_loc = w_q.shape[2] // head_dim
        group_q = q_loc // kv_loc
        prefix = owners * req_pages * page_len
        wanted = page_idx.reshape(owners * req_pages)
        cos_tab, sin_tab = rope_tables(prefix, tokens, head_dim)
        causal = jnp.arange(tokens)[:, None] >= jnp.arange(tokens)[None, :]
        hidden = x_tokens[0]
        for layer_id in range(layers):
            picked = jnp.take(kv_pool[layer_id], wanted, axis=0)
            received = lax.all_to_all(picked, 'pool', 0, 0, tiled=True)
            keys_pre = received[:, 0].reshape(prefix, kv_loc, head_dim)
            vals_pre = received[:, 1].reshape(prefix, kv_loc, head_dim)
            h_att = rms_norm(hidden, gain_attn[layer_id])
            q_proj = jnp.dot(h_att, w_q[layer_id], preferred_element_type=jnp.float32).reshape(tokens, q_loc, head_dim)
            k_proj = jnp.dot(h_att, w_k[layer_id], preferred_element_type=jnp.float32).reshape(tokens, kv_loc, head_dim)
            queries = apply_rope(q_proj, cos_tab, sin_tab).astype(jnp.bfloat16).reshape(tokens, kv_loc, group_q, head_dim)
            k_new = apply_rope(k_proj, cos_tab, sin_tab).astype(jnp.bfloat16)
            v_new = jnp.dot(h_att, w_v[layer_id], preferred_element_type=jnp.float32).astype(jnp.bfloat16).reshape(tokens, kv_loc, head_dim)
            attn_cat = attend(queries, keys_pre, vals_pre, k_new, v_new, causal).reshape(tokens, q_loc * head_dim)
            attn_out = lax.psum(jnp.dot(attn_cat, w_o[layer_id], preferred_element_type=jnp.float32), 'heads')
            x_mid = (hidden.astype(jnp.float32) + attn_out).astype(jnp.bfloat16)
            h_mlp = rms_norm(x_mid, gain_mlp[layer_id])
            gate_proj = jnp.dot(h_mlp, w_gate[layer_id], preferred_element_type=jnp.float32)
            up_proj = jnp.dot(h_mlp, w_up[layer_id], preferred_element_type=jnp.float32)
            act_out = (jax.nn.silu(gate_proj) * up_proj).astype(jnp.bfloat16)
            mlp_out = lax.psum(jnp.dot(act_out, w_down[layer_id], preferred_element_type=jnp.float32), 'heads')
            hidden = (x_mid.astype(jnp.float32) + mlp_out).astype(jnp.bfloat16)
        return hidden[None]

    pool_spec = P(None, ('rep', 'pool'), None, None, 'heads', None)
    index_spec = P('rep', 'pool', None)
    x_spec = P(('rep', 'pool'), None, None)
    gain_spec = P(None, None)
    col_spec = P(None, None, 'heads')
    row_spec = P(None, 'heads', None)
    return jax.shard_map(local_fn, mesh=mesh, in_specs=(pool_spec, index_spec, x_spec, gain_spec, col_spec, col_spec, col_spec, row_spec, gain_spec, col_spec, col_spec, row_spec), out_specs=x_spec, check_vma=False)
```

profile of v0, /device:TPU:97, one launch (start us, length us, event | category | flops | bytes accessed | tf_op | source)
XLA Modules:
  0.0 514.9 jit_solution(10567666212534165465)
XLA Ops:
  6.5 0.7 fusion.60
  7.2 0.7 compare_and_fusion
  7.9 6.5 %gather_fusion = bf16[8,2,128,8,128]{4,3,2,1,0:T(8,128)(2,1)} fusion(bf16[16,2,128,8,128]{4,3,2,1,0:T(8,128)(2,1)} %bitcast.127, s32[1024]{0:T(1024)S(1)} %pad_clamp_fusion), kind=kCustom, calls=%fused_computation | custom fusion | bytes 8388640 | tf_op jit(solution)/shard_map/jit(_take)/gather | solution.py:58
  14.4 0.0 copy-start.2
  14.4 4.7 broadcast_select_fusion
  19.0 6.5 %all-to-all-start = ((bf16[8,2,128,8,128]{4,3,2,1,0:T(8,128)(2,1)}), bf16[8,2,128,8,128]{4,3,2,1,0:T(8,128)(2,1)}, u32[]{:S(2)}, u32[]{:S(2)}) async-start(bf16[8,2,128,8,128]{4,3,2,1,0:T(8,128)(2,1)} %broadcast_select_fusion), calls=%async_computation | async-start | bytes 8388608 | tf_op jit(solution)/shard_map/all_to_all | solution.py:59
  25.5 0.0 all-reduce.3.cloned.1.call-start
  25.5 0.0 copy-done.2
  25.6 3.1 fusion.10
  28.7 9.2 %fusion.44 = bf16[512,1024]{1,0:T(8,128)(2,1)S(1)} fusion(bf16[1,4096,1024]{2,1,0:T(8,128)(2,1)} %param.18, bf16[1,512,4096]{2,1,0:T(8,128)(2,1)} %param.14, f32[4096]{0:T(1024)S(1)} %bitcast.131, f32[512]{0:T(512)S(1)} %add_rsqrt_fusion.1), kind=kOutput, calls=%fused_computation.51 | convolution fusion | flops 4303880192 | bytes 13649920 | tf_op jit(solution)/shard_map/dot_general | solution.py:67
  37.9 11.5 %copy.30 = bf16[1024,4096]{1,0:T(8,128)(2,1)} copy(bf16[1024,4096]{0,1:T(8,128)(2,1)} %bitcast.117) | data formatting | bytes 16777216 | tf_op jit(solution)/shard_map/dot_general | solution.py:64
  49.4 11.3 %copy.29 = bf16[1024,4096]{1,0:T(8,128)(2,1)} copy(bf16[1024,4096]{0,1:T(8,128)(2,1)} %bitcast.118) | data formatting | bytes 16777216 | tf_op jit(solution)/shard_map/dot_general | solution.py:63
  60.7 0.5 copy.31
  61.3 0.0 slice-start.4
  61.3 0.1 iota_compare_fusion
  61.4 0.5 multiply_cosine_fusion
  61.9 0.0 copy-start
  61.9 0.0 slice-start.5
  61.9 9.2 %fusion.31 = f32[512,8,128]{0,2,1:T(8,128)S(1)} fusion(bf16[8,128,4096]{2,1,0:T(8,128)(2,1)} %bitcast.126, bf16[1,512,4096]{2,1,0:T(8,128)(2,1)} %param.14, f32[4096]{0:T(1024)S(1)} %bitcast.132, f32[512]{0:T(512)S(1)} %add_rsqrt_fusion.1), kind=kOutput, calls=%fused_computation.41 | convolution fusion | flops 4303355904 | bytes 14698496 | tf_op jit(solution)/shard_map/dot_general | solution.py:64
  71.1 0.0 slice-done.4
  71.1 0.0 copy-done
  71.1 0.0 slice-done.5
  71.1 4.6 fusion.33
  75.8 0.8 subtract_convert_fusion.1
  76.6 4.7 fusion.26
  81.3 0.0 all-to-all-done
  81.3 2.5 fusion.71
  83.8 0.0 slice-start.2
  83.8 0.5 copy.14
  84.4 0.0 slice-start.3
  84.4 8.1 %bitcast_reduce_fusion = (f32[8,512]{1,0:T(8,128)S(1)}, f32[8,1024,512]{2,1,0:T(8,128)}) fusion(bf16[1024,8,128]{2,0,1:T(8,128)(2,1)S(1)} %bitcast.116, bf16[512,8,64]{0,2,1:T(8,128)(2,1)S(1)} %get-tuple-element.10, bf16[512,8,64]{0,2,1:T(8,128)(2,1)S(1)} %get-tuple-element.9), kind=kOutput, calls=%fused_computation.8 | convolution fusion | flops 1084223488 | bytes 19939328 | tf_op jit(solution)/shard_map/tgrd,ngd->grtn/dot_general | solution.py:29
  92.4 0.0 slice-done.2
  92.4 0.0 slice-done.3
  92.4 1.7 fusion.25
  94.2 8.7 %fusion.7 = f32[8,512]{1,0:T(8,128)S(1)} fusion(f32[8,1024,512]{2,1,0:T(8,128)} %get-tuple-element.18, f32[8,512]{1,0:T(8,128)S(1)} %max.8), kind=kLoop, calls=%fused_computation.11 | loop fusion | flops 12578816 | bytes 16809984 | tf_op jit(solution)/shard_map/reduce_sum | solution.py:35
  102.9 0.0 slice-start
  102.9 6.1 %fusion.36 = f32[8,128,512]{2,1,0:T(8,128)S(1)} fusion(bf16[512,8,128]{0,2,1:T(8,128)(2,1)S(1)} %bitcast.130, f32[8,512,512]{2,1,0:T(8,128)} %get-tuple-element.20, f32[8,512]{1,0:T(8,128)S(1)} %add_divide_fusion, f32[8,512]{1,0:T(8,128)S(1)} %max.8, pred[512,512]{0,1:T(8,128)(4,1)S(1)} %iota_compare_fusion), kind=kOutput, calls=%fused_computation.46 | convolution fusion | flops 547356672 | bytes 11829248 | tf_op jit(solution)/shard_map/grtn,ngd->tgrd/dot_general | solution.py:39
  109.0 0.0 slice-start.1
  109.0 8.2 %add_convert_fusion = bf16[8,128,512]{2,1,0:T(8,128)(2,1)S(1)} fusion(f32[8,128,512]{2,1,0:T(8,128)S(1)} %fusion.36, f32[8,1024,512]{2,1,0:T(8,128)} %get-tuple-element.18, f32[8,512]{1,0:T(8,128)S(1)} %add_divide_fusion, f32[8,512]{1,0:T(8,128)S(1)} %max.8, bf16[1024,8,128]{2,1,0:T(8,128)(2,1)S(1)} %bitcast.128), kind=kOutput, calls=%fused_computation.50 | convolution fusion | flops 1091567616 | bytes 22052864 | tf_op jit(solution)/shard_map/grtn,ngd->tgrd/dot_general | solution.py:38
  117.2 0.0 slice-done
  117.2 0.0 slice-done.1
  117.2 7.0 %fusion.19 = f32[512,4096]{1,0:T(8,128)} fusion(bf16[512,1024]{0,1:T(8,128)(2,1)S(1)} %bitcast.129, bf16[1,1024,4096]{2,1,0:T(8,128)(2,1)S(1)} %bitcast.120), kind=kOutput, calls=%fused_computation.29 | convolution fusion | flops 4294967296 | bytes 17825792 | tf_op jit(solution)/shard_map/dot_general | solution.py:69
  124.2 0.0 copy-start.3
  124.2 0.1 all-reduce.3.cloned.1.call-update
  124.2 0.1 all-reduce.5.cloned.1.call-start
  124.3 0.6 copy-done.3
  124.9 156.4 %all-reduce.3.cloned.1.call-done = f32[512,4096]{1,0:T(8,128)} async-done(((f32[512,4096]{1,0:T(8,128)}), f32[512,4096]{1,0:T(8,128)}) %all-reduce.3.cloned.1.call-update) | async-done | bytes 8388624 | tf_op jit(solution)/shard_map/psum | solution.py:69
  281.3 6.3 %fusion.14 = (f32[512]{0:T(512)S(1)}, bf16[512,4096]{1,0:T(8,128)(2,1)S(1)}) fusion(f32[512,4096]{1,0:T(8,128)} %all-reduce.3.cloned.1.call-done, bf16[1,512,4096]{2,1,0:T(8,128)(2,1)} %param.14), kind=kLoop, calls=%fused_computation.23 | loop fusion | flops 12582400 | bytes 16779264 | tf_op jit(solution)/shard_map/reduce_sum | solution.py:9
  287.6 0.0 copy-start.1
  287.6 19.7 %fusion.4 = f32[512,2752]{0,1:T(8,128)} fusion(bf16[1,4096,2752]{1,2,0:T(8,128)(2,1)} %param.21, bf16[512,4096]{1,0:T(8,128)(2,1)S(1)} %get-tuple-element.6, f32[4096]{0:T(1024)S(1)} %bitcast.134, f32[512]{0:T(512)S(1)} %add_rsqrt_fusion), kind=kOutput, calls=%fused_computation.5 | convolution fusion | flops 11551113216 | bytes 32393216 | tf_op jit(solution)/shard_map/dot_general | solution.py:72
  307.3 0.0 copy-done.1
  307.3 18.4 %multiply_convert_fusion.2.clone.4 = bf16[512,2752]{0,1:T(8,128)(2,1)S(1)} fusion(f32[512,2752]{0,1:T(8,128)} %fusion.4, bf16[1,4096,2752]{1,2,0:T(8,128)(2,1)} %param.22, bf16[512,4096]{1,0:T(8,128)(2,1)S(1)} %get-tuple-element.6, f32[4096]{0:T(1024)S(1)} %bitcast.135, f32[512]{0:T(512)S(1)} %add_rsqrt_fusion), kind=kOutput, calls=%fused_computation.38.clone.clone.clone.1 | convolution fusion | flops 11559567360 | bytes 35211264 | tf_op jit(solution)/shard_map/dot_general | solution.py:73
  325.7 18.9 %fusion = f32[512,4096]{1,0:T(8,128)} fusion(bf16[1,2752,4096]{2,1,0:T(8,128)(2,1)} %param.23, bf16[512,2752]{0,1:T(8,128)(2,1)S(1)} %multiply_convert_fusion.2.clone.4), kind=kOutput, calls=%fused_computation.1 | convolution fusion | flops 11542724608 | bytes 33751040 | tf_op jit(solution)/shard_map/dot_general | solution.py:75
  344.7 0.1 all-reduce.5.cloned.1.call-update
  344.7 154.9 %all-reduce.5.cloned.1.call-done = f32[512,4096]{1,0:T(8,128)} async-done(((f32[512,4096]{1,0:T(8,128)}), f32[512,4096]{1,0:T(8,128)}) %all-reduce.5.cloned.1.call-update) | async-done | bytes 8388624 | tf_op jit(solution)/shard_map/psum | solution.py:75
  499.6 8.0 %fusion.30 = bf16[1,512,4096]{2,1,0:T(8,128)(2,1)} fusion(f32[512,4096]{1,0:T(8,128)} %all-reduce.5.cloned.1.call-done, bf16[512,4096]{1,0:T(8,128)(2,1)} %copy-done.1), kind=kLoop, calls=%fused_computation.40 | loop fusion | flops 6291456 | bytes 16777216 | tf_op jit(solution)/shard_map/broadcast_in_dim | solution.py:77
  (12 shorter events, 0.1 us)
Async XLA Ops:
  14.4 11.2 %copy-start.2 = (bf16[1,4096]{1,0:T(2,128)(2,1)S(1)}, bf16[1,4096]{1,0:T(2,128)(2,1)}, u32[]{:S(2)}) copy-start(bf16[1,4096]{1,0:T(2,128)(2,1)} %param.15) | copy-start | bytes 24580
  19.0 62.3 %all-to-all-start = ((bf16[8,2,128,8,128]{4,3,2,1,0:T(8,128)(2,1)}), bf16[8,2,128,8,128]{4,3,2,1,0:T(8,128)(2,1)}, u32[]{:S(2)}, u32[]{:S(2)}) async-start(bf16[8,2,128,8,128]{4,3,2,1,0:T(8,128)(2,1)} %broadcast_select_fusion), calls=%async_computation | async-start | bytes 8388608 | tf_op jit(solution)/shard_map/all_to_all | solution.py:59
  25.5 255.7 %all-reduce.3.cloned.1.call-start = ((), (), s32[]{:S(2)}) async-start(), calls=%async_computation.1 | async-start | bytes 16777216 | tf_op jit(solution)/shard_map/psum | solution.py:69
  61.3 9.8 %slice-start.4 = ((s8[8388608]{0:T(1024)(128)(4,1)}), s8[4194304]{0:T(1024)(128)(4,1)S(1)}, s32[]{:S(2)}) async-start(s8[8388608]{0:T(1024)(128)(4,1)} %bitcast.123), calls=%async_computation.7 | async-start | bytes 8388608
  61.9 9.2 %copy-start = (bf16[1,512,4096]{2,1,0:T(8,128)(2,1)S(1)}, bf16[1,512,4096]{2,1,0:T(8,128)(2,1)}, u32[]{:S(2)}) copy-start(bf16[1,512,4096]{2,1,0:T(8,128)(2,1)} %param.14) | copy-start | bytes 12582916
  61.9 9.2 %slice-start.5 = ((s8[8388608]{0:T(1024)(128)(4,1)}), s8[4194304]{0:T(1024)(128)(4,1)S(1)}, s32[]{:S(2)}) async-start(s8[8388608]{0:T(1024)(128)(4,1)} %bitcast.123), calls=%async_computation.8 | async-start | bytes 8388608
  83.8 8.6 %slice-start.2 = ((s8[8388608]{0:T(1024)(128)(4,1)}), s8[4194304]{0:T(1024)(128)(4,1)S(1)}, s32[]{:S(2)}) async-start(s8[8388608]{0:T(1024)(128)(4,1)} %bitcast.121), calls=%async_computation.5 | async-start | bytes 8388608
  84.4 8.1 %slice-start.3 = ((s8[8388608]{0:T(1024)(128)(4,1)}), s8[4194304]{0:T(1024)(128)(4,1)S(1)}, s32[]{:S(2)}) async-start(s8[8388608]{0:T(1024)(128)(4,1)} %bitcast.121), calls=%async_computation.6 | async-start | bytes 8388608
  102.9 14.3 %slice-start = ((s8[8388608]{0:T(1024)(128)(4,1)}), s8[4194304]{0:T(1024)(128)(4,1)S(1)}, s32[]{:S(2)}) async-start(s8[8388608]{0:T(1024)(128)(4,1)} %bitcast.119), calls=%async_computation.3 | async-start | bytes 8388608
  109.0 8.2 %slice-start.1 = ((s8[8388608]{0:T(1024)(128)(4,1)}), s8[4194304]{0:T(1024)(128)(4,1)S(1)}, s32[]{:S(2)}) async-start(s8[8388608]{0:T(1024)(128)(4,1)} %bitcast.119), calls=%async_computation.4 | async-start | bytes 8388608
  124.2 0.7 copy-start.3
  124.2 375.4 %all-reduce.5.cloned.1.call-start = ((), (), s32[]{:S(2)}) async-start(), calls=%async_computation.2 | async-start | bytes 16777216 | tf_op jit(solution)/shard_map/psum | solution.py:75
  287.6 19.8 %copy-start.1 = (bf16[512,4096]{1,0:T(8,128)(2,1)}, bf16[512,4096]{1,0:T(8,128)(2,1)S(1)}, u32[]{:S(2)}) copy-start(bf16[512,4096]{1,0:T(8,128)(2,1)S(1)} %get-tuple-element.6) | copy-start | bytes 12582916
Sparse Core Ops, SparseCore 0:
  124.4 156.8 all-reduce.2
  344.9 154.7 all-reduce.4
where the time goes:
time: 522 us; the launch traced here: 515 us
  waiting for transfers between devices  311 us (60%)
  matrix products  114 us (22%)
  other arithmetic  35.2 us (7%)
  local copies, waits for them, and re-layouts  33.5 us (6%)
  between operations  14.1 us (3%)
  starting transfers between devices  6.57 us (1%)
    psum x1, waiting for transfers between devices, local_fn(): lax.psum(jnp.dot(attn_cat, w_o[layer_id], preferred_element_type=jnp.floa...  156 us
    psum x1, waiting for transfers between devices, local_fn(): lax.psum(jnp.dot(act_out, w_down[layer_id], preferred_element_type=jnp.fl...  155 us
    dot_general x1, matrix products, local_fn(): jnp.dot(h_mlp, w_gate[layer_id], preferred_element_type=jnp.float32)  19.7 us
    dot_general x1, matrix products, local_fn(): jnp.dot(act_out, w_down[layer_id], preferred_element_type=jnp.float32)  18.9 us
    dot_general x1, matrix products, local_fn(): up_proj = jnp.dot(h_mlp, w_up[layer_id], preferred_element_type=jnp.float32)  18.4 us
    dot_general x1, local copies, waits for them, and re-layouts, local_fn(): jnp.dot(h_att, w_k[layer_id], preferred_element_type=jnp.float32)  11.5 us
    dot_general x1, local copies, waits for them, and re-layouts, local_fn(): jnp.dot(h_att, w_q[layer_id], preferred_element_type=jnp.float32)  11.3 us
  transfers between devices with their start and end apart: 3, of which 2 were waited for; matrix products, arithmetic and copies ran while one was open for 11% of the time, Pallas kernels for 0%

commit v1 on v0

v1 whole, which is shorter than its diff:
```python
import functools

import jax
import jax.numpy as jnp
from jax import lax
from jax.experimental import pallas as pl
from jax.experimental.pallas import tpu as pltpu
from jax.sharding import PartitionSpec as P

MESH = pl.DeviceIdType.MESH
BF16 = jnp.bfloat16
F32 = jnp.float32
ANY = pl.BlockSpec(memory_space=pl.ANY)
VMEM_MAX = 67043328


def rms_norm(hidden, gain_vec):
    hid_f32 = hidden.astype(F32)
    inv_rms = lax.rsqrt(jnp.mean(hid_f32 * hid_f32, axis=-1, keepdims=True) + 1e-5)
    return (hid_f32 * inv_rms * gain_vec.astype(F32)).astype(BF16)


def rope_tables(prefix, tokens, head_dim):
    positions = (prefix + jnp.arange(tokens)).astype(F32)
    inv_freq = 10000.0 ** (-2.0 * jnp.arange(head_dim // 2).astype(F32) / head_dim)
    angles = positions[:, None] * inv_freq[None, :]
    cos_half, sin_half = jnp.cos(angles), jnp.sin(angles)
    return jnp.concatenate([cos_half, cos_half], axis=-1), jnp.concatenate([-sin_half, sin_half], axis=-1)


def ring_neighbours(axis, size):
    me = lax.axis_index(axis)
    return me, lax.rem(me + 1, size), lax.rem(me + size - 1, size)


def greet(left, right):
    barrier = pltpu.get_barrier_semaphore()
    for neighbour in (left, right):
        pl.semaphore_signal(barrier, inc=1, device_id={"heads": neighbour}, device_id_type=MESH)
    pl.semaphore_wait(barrier, 2)


def remote(src, dst, send_sem, recv_sem, target):
    return pltpu.make_async_remote_copy(
        src_ref=src, dst_ref=dst, send_sem=send_sem, recv_sem=recv_sem, device_id={"heads": target}, device_id_type=MESH
    )


def attend_kernel(ring, head_dim, heads, q_ref, k_ref, v_ref, kv_ref, cos_ref, sin_ref, out_ref, gathered, send_sem, recv_sem, out_sem):
    me, right, left = ring_neighbours("heads", ring)
    tokens = q_ref.shape[0]
    half = tokens // 2
    prefix = kv_ref.shape[0] * kv_ref.shape[3]
    scale = head_dim ** -0.5
    nt = (((1,), (1,)), ((), ()))
    greet(left, right)

    def lanes(g):
        return pl.ds(pl.multiple_of(g * head_dim, head_dim), head_dim)

    def direct(g, way):
        piece = gathered.at[me, :, lanes(g)]
        return remote(piece, piece, send_sem.at[g, 0, way], recv_sem.at[g, 0, way], (right, left)[way])

    def passed(g, way):
        rows = pl.ds(way * half, half)
        piece = gathered.at[(left, right)[way], rows, lanes(g)]
        return remote(piece, piece, send_sem.at[g, 1, way], recv_sem.at[g, 1, way], (right, left)[way])

    def forward(g):
        for way in range(2):
            direct(g, way).wait_recv()
            passed(g, way).start()

    def rope(ref, g):
        val = ref[:, lanes(g)]
        return (val * cos_ref[...] + pltpu.roll(val, head_dim // 2, 1) * sin_ref[...]).astype(BF16)

    def one_head(g, carry):
        queries, keys_new = rope(q_ref, g), rope(k_ref, g)
        keys_pre = kv_ref[:, g, 0].reshape(prefix, head_dim)
        vals_pre = kv_ref[:, g, 1].reshape(prefix, head_dim)
        vals_new = v_ref[:, lanes(g)]
        for part in range(2):
            rows = slice(part * half, (part + 1) * half)
            seen = (part + 1) * half
            q_part = queries[rows]
            s_pre = lax.dot_general(q_part, keys_pre, nt, preferred_element_type=F32) * scale
            s_new = lax.dot_general(q_part, keys_new[:seen], nt, preferred_element_type=F32) * scale
            t_id = lax.broadcasted_iota(jnp.int32, s_new.shape, 0) + part * half
            u_id = lax.broadcasted_iota(jnp.int32, s_new.shape, 1)
            s_new = jnp.where(t_id >= u_id, s_new, -jnp.inf)
            row_max = jnp.maximum(jnp.max(s_pre, axis=-1, keepdims=True), jnp.max(s_new, axis=-1, keepdims=True))
            e_pre = jnp.exp(s_pre - row_max)
            e_new = jnp.exp(s_new - row_max)
            inv_den = 1.0 / (jnp.sum(e_pre, axis=-1, keepdims=True) + jnp.sum(e_new, axis=-1, keepdims=True))
            total = jnp.dot((e_pre * inv_den).astype(BF16), vals_pre, preferred_element_type=F32)
            total = total + jnp.dot((e_new * inv_den).astype(BF16), vals_new[:seen], preferred_element_type=F32)
            gathered[me, rows, lanes(g)] = total.astype(BF16)
        for way in range(2):
            direct(g, way).start()

        @pl.when(g > 0)
        def _():
            forward(g - 1)

        return carry

    lax.fori_loop(0, heads, one_head, 0)
    forward(heads - 1)

    def settle(g, carry):
        for way in range(2):
            direct(g, way).wait_send()
            passed(g, way).wait()
        return carry

    lax.fori_loop(0, heads, settle, 0)
    copy = pltpu.make_async_copy(gathered, out_ref, out_sem)
    copy.start()
    copy.wait()


def attend(call_id, ring, part, heads, head_dim, q, k, v, kv, cos_tab, sin_tab):
    tokens = q.shape[0]
    width = heads * head_dim
    cols = pl.BlockSpec((tokens, width), lambda i: (0, part))
    whole = lambda arr: pl.BlockSpec(arr.shape, lambda i: (0,) * arr.ndim)
    keys = kv.shape[0] * kv.shape[3] + tokens
    return pl.pallas_call(
        functools.partial(attend_kernel, ring, head_dim, heads),
        grid=(1,),
        out_shape=jax.ShapeDtypeStruct((ring, tokens, width), BF16),
        in_specs=[cols, cols, cols, whole(kv), whole(cos_tab), whole(sin_tab)],
        out_specs=ANY,
        scratch_shapes=[
            pltpu.VMEM((ring, tokens, width), BF16),
            pltpu.SemaphoreType.DMA((heads, 2, 2)),
            pltpu.SemaphoreType.DMA((heads, 2, 2)),
            pltpu.SemaphoreType.DMA,
        ],
        compiler_params=pltpu.CompilerParams(collective_id=call_id, has_side_effects=True, vmem_limit_bytes=48 * 2**20),
        cost_estimate=pl.CostEstimate(flops=16 * width * tokens * keys, bytes_accessed=8 * 2**20, transcendentals=heads * tokens * keys),
        name=f"attend_{part}",
    )(q, k, v, kv, cos_tab, sin_tab)


CHUNKS = 2
GROUPS = 4
K_BLOCK = 512


def mlp_kernel(ring, core, a0_ref, a1_ref, wm_ref, wo_ref, x_ref, gain_ref, wg_ref, wu_ref, wd_ref, out_ref,
               mid, normed, gate_w, up_w, part_sum, running, result,
               local_sem, w_sem, d_sem, mid_send, mid_recv, rs_send, rs_recv, ag_send, ag_recv, out_sem):
    me, right, left = ring_neighbours("heads", ring)
    ways = (right, left)
    half_id = core()
    tokens, width = x_ref.shape
    block = width // ring
    hid = wg_ref.shape[1]
    rows_c = tokens // CHUNKS
    rows_g = tokens // GROUPS
    per_chunk = GROUPS // CHUNKS
    k_steps = width // K_BLOCK
    n_half = block // 2
    a_cols = a0_ref.shape[2]

    def load_gate_up(kk):
        rows = pl.ds(pl.multiple_of(lax.rem(kk, k_steps) * K_BLOCK, K_BLOCK), K_BLOCK)
        slot = lax.rem(kk, 2)
        return (pltpu.make_async_copy(wg_ref.at[rows], gate_w.at[slot], w_sem.at[0, slot]),
                pltpu.make_async_copy(wu_ref.at[rows], up_w.at[slot], w_sem.at[1, slot]))

    for copy in load_gate_up(0):
        copy.start()

    greet(left, right)

    def mid_direct(c, way):
        piece = mid.at[me, pl.ds(c * rows_c, rows_c)]
        return remote(piece, piece, mid_send.at[c, 0, way], mid_recv.at[c, 0, way], ways[way])

    def mid_passed(c, way):
        piece = mid.at[(left, right)[way], pl.ds(c * rows_c + way * (rows_c // 2), rows_c // 2)]
        return remote(piece, piece, mid_send.at[c, 1, way], mid_recv.at[c, 1, way], ways[way])

    def mid_forward(c):
        for way in range(2):
            mid_direct(c, way).wait_recv()
            mid_passed(c, way).start()

    def output_product(a_buf, w_buf, x_buf):
        copies = [
            pltpu.make_async_copy(a0_ref, a_buf.at[0], local_sem.at[0]),
            pltpu.make_async_copy(a1_ref, a_buf.at[1], local_sem.at[1]),
            pltpu.make_async_copy(wm_ref, w_buf.at[half_id], local_sem.at[2]),
            pltpu.make_async_copy(wo_ref, w_buf.at[1 - half_id], local_sem.at[3]),
            pltpu.make_async_copy(x_ref.at[:, pl.ds(pl.multiple_of(me * block, block), block)], x_buf, local_sem.at[4]),
        ]
        for copy in copies:
            copy.start()
        for copy in copies:
            copy.wait()
        for c in range(CHUNKS):
            for n in range(2):
                cols = slice(n * n_half, (n + 1) * n_half)
                rows = slice(c * rows_c, (c + 1) * rows_c)
                total = jnp.zeros((rows_c, n_half), F32)
                for hf in range(2):
                    for src in range(ring):
                        total = total + jnp.dot(a_buf[hf, src, rows], w_buf[hf, src, :, cols], preferred_element_type=F32)
                mid[me, rows, cols] = (x_buf[rows, cols].astype(F32) + total).astype(BF16)
            if c > 0:
                mid_forward(c - 1)
            for way in range(2):
                mid_direct(c, way).start()

    pl.run_scoped(
        output_product,
        pltpu.VMEM((2, ring, tokens, a_cols), BF16),
        pltpu.VMEM((2, ring, a_cols, block), BF16),
        pltpu.VMEM((tokens, block), BF16),
    )

    def mid_settle(c):
        for way in range(2):
            mid_passed(c, way).wait_recv()

    def rs_block(s, way):
        return lax.rem(me + ring - 1 - s, ring) if way == 0 else lax.rem(me + 1 + s, ring)

    def rs_send_copy(r, s, way):
        rows = pl.ds((r % per_chunk) * rows_g, rows_g)
        src = part_sum.at[r // per_chunk, 0, way, rows] if s == 0 else running.at[r, s - 1, way]
        return remote(src, running.at[r, s, way], rs_send.at[r, s, way], rs_recv.at[r, s, way], ways[way])

    def rs_step(r, s):
        rows = slice((r % per_chunk) * rows_g, (r % per_chunk + 1) * rows_g)
        for way in range(2):
            rs_send_copy(r, s - 1, way).wait_recv()
            running[r, s - 1, way] = running[r, s - 1, way] + part_sum[r // per_chunk, s, way, rows]
            rs_send_copy(r, s, way).start()

    def ag_direct(r, way):
        piece = result.at[me, pl.ds(r * rows_g, rows_g)]
        return remote(piece, piece, ag_send.at[r, 0, way], ag_recv.at[r, 0, way], ways[way])

    def ag_passed(r, way):
        piece = result.at[(left, right)[way], pl.ds(r * rows_g + way * (rows_g // 2), rows_g // 2)]
        return remote(piece, piece, ag_send.at[r, 1, way], ag_recv.at[r, 1, way], ways[way])

    def rs_final(r):
        rows = slice((r % per_chunk) * rows_g, (r % per_chunk + 1) * rows_g)
        dst = slice(r * rows_g, (r + 1) * rows_g)
        for way in range(2):
            rs_send_copy(r, ring - 2, way).wait_recv()
            cols = slice(way * n_half, (way + 1) * n_half)
            total = running[r, ring - 2, way] + part_sum[r // per_chunk, ring - 1, way, rows]
            result[me, dst, cols] = (mid[me, dst, cols].astype(F32) + total).astype(BF16)
        for way in range(2):
            ag_direct(r, way).start()

    def ag_forward(r):
        for way in range(2):
            ag_direct(r, way).wait_recv()
            ag_passed(r, way).start()

    def put_out(r, src):
        rows = pl.ds(r * rows_g, rows_g)
        cols = pl.ds(src * block, block)
        return pltpu.make_async_copy(result.at[src, rows], out_ref.at[rows, cols], out_sem.at[r, src])

    def ag_settle(r):
        for way in range(2):
            ag_passed(r, way).wait_recv()
        for src in range(ring):
            put_out(r, src).start()

    def hidden_part(acc_g, acc_u, act, down_w, gain_buf):
        gain_copy = pltpu.make_async_copy(gain_ref, gain_buf, local_sem.at[0])
        gain_copy.start()
        gain_copy.wait()

        def load_down(jj):
            s, way = lax.rem(jj // 2, ring), lax.rem(jj, 2)
            blk = jnp.where(way == 0, lax.rem(me + 2 * ring - 1 - s, ring), lax.rem(me + 1 + s, ring))
            col = pl.multiple_of(blk * block + way * n_half, n_half)
            slot = lax.rem(jj, 3)
            return pltpu.make_async_copy(wd_ref.at[:, pl.ds(col, n_half)], down_w.at[slot], d_sem.at[slot])

        for jj in range(2):
            load_down(jj).start()

        def normalise(c):
            for sub in range(rows_c // 128):
                rows = slice(c * rows_c + sub * 128, c * rows_c + (sub + 1) * 128)
                squares = jnp.zeros((128, 1), F32)
                for b in range(ring):
                    val = mid[b, rows].astype(F32)
                    squares = squares + jnp.sum(val * val, axis=-1, keepdims=True)
                inv_rms = lax.rsqrt(squares * (1.0 / width) + 1e-5)
                for b in range(ring):
                    gain = gain_buf[:, b * block:(b + 1) * block].astype(F32)
                    normed[b, sub * 128:(sub + 1) * 128] = (mid[b, rows].astype(F32) * inv_rms * gain).astype(BF16)

        def gate_up(c, tasks):
            acc_g[...] = jnp.zeros(acc_g.shape, F32)
            acc_u[...] = jnp.zeros(acc_u.shape, F32)
            per_block = block // K_BLOCK

            def body(kb, carry):
                kk = c * k_steps + kb
                slot = lax.rem(kk, 2)
                loaded = load_gate_up(kk)
                for copy in loaded:
                    copy.wait()

                @pl.when(kk + 1 < CHUNKS * k_steps)
                def _():
                    for copy in load_gate_up(kk + 1):
                        copy.start()

                lhs = normed[kb // per_block, :, pl.ds(pl.multiple_of(lax.rem(kb, per_block) * K_BLOCK, K_BLOCK), K_BLOCK)]
                acc_g[...] += jnp.dot(lhs, gate_w[slot], preferred_element_type=F32)
                acc_u[...] += jnp.dot(lhs, up_w[slot], preferred_element_type=F32)
                for at, task in tasks:
                    pl.when(kb == at)(task)
                return carry

            lax.fori_loop(0, k_steps, body, 0)
            for sub in range(rows_c // 32):
                rows = slice(sub * 32, (sub + 1) * 32)
                gate = acc_g[rows]
                act[rows] = (gate * jax.nn.sigmoid(gate) * acc_u[rows]).astype(BF16)

        def down(c, tasks):
            def body(s, carry):
                for way in range(2):
                    jj = c * 2 * ring + 2 * s + way
                    load_down(jj).wait()

                    @pl.when(jj + 2 < CHUNKS * 2 * ring)
                    def _():
                        load_down(jj + 2).start()

                    part_sum[c, s, way] = jnp.dot(act[...], down_w[lax.rem(jj, 3)], preferred_element_type=F32)

                @pl.when(s == 0)
                def _():
                    for sub in range(per_chunk):
                        for way in range(2):
                            rs_send_copy(c * per_chunk + sub, 0, way).start()

                for at, task in tasks:
                    pl.when(s == at)(task)
                return carry

            lax.fori_loop(0, ring, body, 0)

        do = functools.partial
        mid_settle(0)
        normalise(0)
        gate_up(0, [(4, do(mid_forward, 1))])
        down(0, [])
        mid_settle(1)
        normalise(1)
        gate_up(1, [(1, do(rs_step, 0, 1)), (3, do(rs_step, 1, 1)), (5, do(rs_step, 0, 2)), (7, do(rs_step, 1, 2))])
        down(1, [(1, do(rs_final, 0)), (3, do(rs_final, 1))])

    pl.run_scoped(
        hidden_part,
        pltpu.VMEM((rows_c, hid), F32),
        pltpu.VMEM((rows_c, hid), F32),
        pltpu.VMEM((rows_c, hid), BF16),
        pltpu.VMEM((3, hid, n_half), BF16),
        pltpu.VMEM((1, width), BF16),
    )

    rs_step(2, 1)
    rs_step(3, 1)
    ag_forward(0)
    rs_step(2, 2)
    ag_forward(1)
    rs_step(3, 2)
    rs_final(2)
    rs_final(3)
    ag_settle(0)
    ag_settle(1)
    ag_forward(2)
    ag_forward(3)
    ag_settle(2)
    ag_settle(3)
    for c in range(CHUNKS):
        for way in range(2):
            mid_direct(c, way).wait_send()
            mid_passed(c, way).wait_send()
    for r in range(GROUPS):
        for way in range(2):
            for s in range(ring - 1):
                rs_send_copy(r, s, way).wait_send()
            ag_direct(r, way).wait_send()
            ag_passed(r, way).wait_send()
        for src in range(ring):
            put_out(r, src).wait()


def mlp(call_id, ring, core, a0, a1, w_mine, w_other, x, gain, w_gate, w_up, w_down):
    tokens, width = x.shape
    hid = w_gate.shape[1]
    block = width // ring
    rows_c, rows_g = tokens // CHUNKS, tokens // GROUPS
    dma = pltpu.SemaphoreType.DMA
    return pl.pallas_call(
        functools.partial(mlp_kernel, ring, core),
        out_shape=jax.ShapeDtypeStruct((tokens, width), BF16),
        in_specs=[ANY] * 9,
        out_specs=ANY,
        scratch_shapes=[
            pltpu.VMEM((ring, tokens, block), BF16),
            pltpu.VMEM((ring, rows_c, block), BF16),
            pltpu.VMEM((2, K_BLOCK, hid), BF16),
            pltpu.VMEM((2, K_BLOCK, hid), BF16),
            pltpu.VMEM((CHUNKS, ring, 2, rows_c, block // 2), F32),
            pltpu.VMEM((GROUPS, ring - 1, 2, rows_g, block // 2), F32),
            pltpu.VMEM((ring, tokens, block), BF16),
            dma((5,)), dma((2, 2)), dma((3,)),
            dma((CHUNKS, 2, 2)), dma((CHUNKS, 2, 2)),
            dma((GROUPS, ring - 1, 2)), dma((GROUPS, ring - 1, 2)),
            dma((GROUPS, 2, 2)), dma((GROUPS, 2, 2)),
            dma((GROUPS, ring)),
        ],
        compiler_params=pltpu.CompilerParams(collective_id=call_id, has_side_effects=True, vmem_limit_bytes=VMEM_MAX),
        cost_estimate=pl.CostEstimate(flops=2 * tokens * width * (block + 3 * hid), bytes_accessed=160 * 2**20, transcendentals=tokens * hid),
        name="mlp",
    )(a0, a1, w_mine, w_other, x, gain, w_gate, w_up, w_down)


def solution(mesh):
    owners = mesh.shape["pool"]
    ring = mesh.shape["heads"]
    assert ring == 4 and owners % 2 == 0

    def local_fn(kv_pool, page_idx, x_tokens, gain_attn, w_q, w_k, w_v, w_o, gain_mlp, w_gate, w_up, w_down):
        layers, _, _, page_len, kv_loc, head_dim = kv_pool.shape
        tokens, width = x_tokens.shape[1:]
        req_pages = page_idx.shape[2]
        prefix = owners * req_pages * page_len
        wanted = page_idx.reshape(owners * req_pages)
        cos_tab, sin_tab = rope_tables(prefix, tokens, head_dim)
        core = lambda: lax.rem(lax.axis_index("pool"), 2)
        swap = [(i, i ^ 1) for i in range(owners)]
        hidden = x_tokens[0]
        heads = kv_loc // 2
        for layer in range(layers):
            picked = kv_pool.at[layer, wanted].get(mode="promise_in_bounds").transpose(0, 3, 1, 2, 4)
            rows_half = w_o.shape[1] // 2
            mine = lax.dynamic_slice_in_dim(w_o[layer], core() * rows_half, rows_half, 0)
            mine = mine.reshape(rows_half, ring, width // ring).transpose(1, 0, 2)
            received = [lax.all_to_all(picked[:, p * heads:(p + 1) * heads], "pool", 0, 0, tiled=True) for p in range(2)]
            wo_mine = lax.all_to_all(mine, "heads", 0, 0, tiled=True)
            wo_other = lax.ppermute(wo_mine, "pool", swap)
            h_att = rms_norm(hidden, gain_attn[layer])
            q = jnp.dot(h_att, w_q[layer], preferred_element_type=F32)
            k = jnp.dot(h_att, w_k[layer], preferred_element_type=F32)
            v = jnp.dot(h_att, w_v[layer], preferred_element_type=F32).astype(BF16)
            a0, a1 = (attend(3 * layer + p, ring, p, heads, head_dim, q, k, v, received[p], cos_tab, sin_tab) for p in range(2))
            hidden = mlp(3 * layer + 2, ring, core, a0, a1, wo_mine, wo_other, hidden, gain_mlp[layer][None], w_gate[layer], w_up[layer], w_down[layer])
        return hidden[None]

    pool_spec = P(None, ("rep", "pool"), None, None, "heads", None)
    index_spec = P("rep", "pool", None)
    x_spec = P(("rep", "pool"), None, None)
    gain_spec = P(None, None)
    col_spec = P(None, None, "heads")
    row_spec = P(None, "heads", None)
    return jax.shard_map(local_fn, mesh=mesh, in_specs=(pool_spec, index_spec, x_spec, gain_spec, col_spec, col_spec, col_spec, row_spec, gain_spec, col_spec, col_spec, row_spec), out_specs=x_spec, check_vma=False)
```

time: 522 us -> 376 us (0.72)
  waiting for transfers between devices: 311 us -> 14.2 us
  Pallas kernels: 0 us -> 204 us
  matrix products: 114 us -> 27 us
  local copies, waits for them, and re-layouts: 33.5 us -> 101 us
  other arithmetic: 35.2 us -> 4.47 us
  between operations: 14.1 us -> 0.12 us
  starting transfers between devices: 6.57 us -> 17.7 us
    psum x2 -> x0, waiting for transfers between devices: 311 us -> none  [the longest x1 156 us: local_fn(): lax.psum(jnp.dot(attn_cat, w_o[layer_id], preferred_element_type=jnp.floa...]
    pallas_call x0 -> x3, Pallas kernels: none -> 204 us  [the longest x1 155 us: mlp(): pl.pallas_call(functools.partial(mlp_kernel, ring, core), out_shape=jax.S...]
    dot_general x11 -> x3, matrix products: 114 us -> 27 us  [the longest x1 10.5 us: local_fn(): k = jnp.dot(h_att, w_k[layer], preferred_element_type=F32)]
    unnamed x20 -> x22, local copies, waits for them, and re-layouts: 0.63 us -> 75.2 us
    dot_general x2 -> x0, local copies, waits for them, and re-layouts: 22.8 us -> none  [the longest x1 11.5 us: local_fn(): jnp.dot(h_att, w_k[layer_id], preferred_element_type=jnp.float32)]
    all_to_all x1 -> x3, waiting for transfers between devices: 0.01 us -> 14.2 us  [the longest x2 14.2 us: local_fn(): lax.all_to_all(picked[:, p * heads:(p + 1) * heads], 'pool', 0, 0, tiled=...]
    all_to_all x1 -> x3, starting transfers between devices: 6.5 us -> 17.5 us  [the longest x2 10.9 us: local_fn(): lax.all_to_all(picked[:, p * heads:(p + 1) * heads], 'pool', 0, 0, tiled=...]
    reduce_sum x2 -> x0, other arithmetic: 10.4 us -> none  [the longest x1 8.67 us: attend(): jnp.sum(e_pre, axis=-1, keepdims=True)]
  transfers between devices with their start and end apart: 3 -> 4, of which waited for: 2 -> 1; matrix products, arithmetic and copies ran while one was open for 11% -> 28% of each run, Pallas kernels for 0% -> 13%
where the time goes in v1:
time: 376 us; the launch traced here: 368 us
  Pallas kernels  204 us (54%)
  local copies, waits for them, and re-layouts  101 us (27%)
  matrix products  27 us (7%)
  starting transfers between devices  17.7 us (5%)
  waiting for transfers between devices  14.2 us (4%)
  other arithmetic  4.47 us (1%)
    pallas_call x1, Pallas kernels, mlp(): pl.pallas_call(functools.partial(mlp_kernel, ring, core), out_shape=jax.S...  155 us
    unnamed x22, local copies, waits for them, and re-layouts  75.2 us
    pallas_call x2, Pallas kernels, attend(): pl.pallas_call(functools.partial(attend_kernel, ring, head_dim, heads), g...  49.6 us
    all_to_all x2, waiting for transfers between devices, local_fn(): lax.all_to_all(picked[:, p * heads:(p + 1) * heads], 'pool', 0, 0, tiled=...  14.2 us
    gather x2, local copies, waits for them, and re-layouts, local_fn(): kv_pool.at[layer, wanted].get(mode='promise_in_bounds')  11.8 us
    all_to_all x2, starting transfers between devices, local_fn(): lax.all_to_all(picked[:, p * heads:(p + 1) * heads], 'pool', 0, 0, tiled=...  10.9 us
    dot_general x1, matrix products, local_fn(): k = jnp.dot(h_att, w_k[layer], preferred_element_type=F32)  10.5 us
    dot_general x1, matrix products, local_fn(): q = jnp.dot(h_att, w_q[layer], preferred_element_type=F32)  8.31 us
  transfers between devices with their start and end apart: 4, of which 1 were waited for; matrix products, arithmetic and copies ran while one was open for 28% of the time, Pallas kernels for 13%

profile of v1, /device:TPU:97, one launch (start us, length us, event | category | flops | bytes accessed | tf_op | source)
XLA Modules:
  0.0 368.4 jit_solution(4241363950837205426)
XLA Ops:
  0.0 4.7 %constant_dynamic-slice_fusion = bf16[1,512,4096]{2,1,0:T(8,128)(2,1)} fusion(bf16[1,1024,4096]{2,1,0:T(8,128)(2,1)} %param.19, s32[]{:T(128)S(6)} %select_n.14), kind=kLoop, calls=%fused_computation.24 | loop fusion | bytes 8388612 | tf_op jit(solution)/shard_map/dynamic_slice | solution.py:458
  4.7 6.5 %copy.20 = bf16[1,512,4096]{1,2,0:T(8,128)(2,1)} copy(bf16[1,512,4096]{2,1,0:T(8,128)(2,1)} %constant_dynamic-slice_fusion) | data formatting | bytes 8388608
  11.2 6.3 %copy.17 = bf16[512,4,1024]{2,0,1:T(8,128)(2,1)} copy(bf16[512,4,1024]{0,2,1:T(8,128)(2,1)} %bitcast.36) | data formatting | bytes 8388608 | tf_op jit(solution)/shard_map/reshape | solution.py:459
  17.5 0.0 copy-start.7
  17.5 0.0 copy-start.8
  17.5 6.6 %all-to-all-start.2 = ((bf16[4,512,1024]{2,1,0:T(8,128)(2,1)}), bf16[4,512,1024]{2,1,0:T(8,128)(2,1)}, u32[]{:S(2)}, u32[]{:S(2)}) async-start(bf16[4,512,1024]{2,1,0:T(8,128)(2,1)} %bitcast.34), calls=%async_computation.2 | async-start | bytes 8388608 | tf_op jit(solution)/shard_map/all_to_all | solution.py:461
  24.1 0.0 copy-done.7
  24.1 0.0 copy-done.8
  24.1 6.5 %gather_fusion = bf16[8,2,128,8,128]{4,3,2,1,0:T(8,128)(2,1)} fusion(bf16[1,16,2,128,8,128]{5,4,3,2,1,0:T(8,128)(2,1)} %param.12, s32[8]{0:T(128)S(1)} %fusion.13), kind=kCustom, calls=%fused_computation | custom fusion | bytes 8388672 | tf_op jit(solution)/shard_map/gather | solution.py:456
  30.6 5.3 %copy.22 = bf16[8,2,128,8,128]{4,2,1,3,0:T(8,128)(2,1)} copy(bf16[8,2,128,8,128]{4,3,2,1,0:T(8,128)(2,1)} %gather_fusion) | data formatting | bytes 8388608 | tf_op jit(solution)/shard_map/gather | solution.py:456
  35.9 28.8 %copy.18 = bf16[1,4096,2752]{2,1,0:T(8,128)(2,1)} copy(bf16[1,4096,2752]{1,2,0:T(8,128)(2,1)} %param.21) | data formatting | bytes 45088768 | tf_op args[9]
  64.8 28.6 %copy.19 = bf16[1,4096,2752]{2,1,0:T(8,128)(2,1)} copy(bf16[1,4096,2752]{1,2,0:T(8,128)(2,1)} %param.22) | data formatting | bytes 45088768 | tf_op args[10]
  93.4 0.0 copy-start.4
  93.4 3.2 multiply_reduce_fusion
  96.6 0.2 copy-done.4
  96.8 0.0 copy-start.5
  96.8 2.7 fusion.17
  99.5 1.0 copy-done.5
  100.5 8.2 %fusion.7.v_ref = bf16[512,1024]{1,0:T(8,128)(2,1)} fusion(bf16[1,4096,1024]{2,1,0:T(8,128)(2,1)} %param.18, bf16[1,512,4096]{2,1,0:T(8,128)(2,1)S(1)} %copy-done.5, f32[4096]{0:T(1024)S(1)} %bitcast.39, f32[512]{0:T(512)S(1)} %add_rsqrt_fusion), kind=kOutput, calls=%fused_computation.11 | convolution fusion | flops 4303880192 | bytes 13649920 | tf_op jit(solution)/shard_map/dot_general | solution.py:466
  108.7 0.0 all-to-all-done.2.wm_ref
  108.7 5.5 %all-to-all-start.1 = ((bf16[8,4,2,128,128]{4,3,2,1,0:T(8,128)(2,1)}), bf16[8,4,2,128,128]{4,3,2,1,0:T(8,128)(2,1)S(1)}, u32[]{:S(2)}, u32[]{:S(2)}) async-start(bf16[8,4,2,128,128]{4,3,2,1,0:T(8,128)(2,1)} %get-tuple-element.5), calls=%async_computation.1 | async-start | bytes 4194304 | tf_op jit(solution)/shard_map/all_to_all | solution.py:460
  114.2 1.0 fusion.10
  115.2 0.2 pad_maximum_fusion
  115.4 0.1 collective-permute-start
  115.5 10.5 %fusion.2.k_ref = f32[512,1024]{1,0:T(8,128)} fusion(bf16[1,4096,1024]{2,1,0:T(8,128)(2,1)} %param.17, bf16[1,512,4096]{2,1,0:T(8,128)(2,1)} %param.14, f32[4096]{0:T(1024)S(1)} %bitcast.40, f32[512]{0:T(512)S(1)} %add_rsqrt_fusion), kind=kOutput, calls=%fused_computation.3 | convolution fusion | flops 4303355904 | bytes 14698496 | tf_op jit(solution)/shard_map/dot_general | solution.py:465
  126.0 14.1 %all-to-all-done.1.kv_ref = bf16[8,4,2,128,128]{4,3,2,1,0:T(8,128)(2,1)S(1)} async-done(((bf16[8,4,2,128,128]{4,3,2,1,0:T(8,128)(2,1)}), bf16[8,4,2,128,128]{4,3,2,1,0:T(8,128)(2,1)S(1)}, u32[]{:S(2)}, u32[]{:S(2)}) %all-to-all-start.1) | async-done | bytes 2097184 | tf_op jit(solution)/shard_map/all_to_all | solution.py:460
  140.2 0.0 copy-start.6
  140.2 1.4 copy-done.6
  141.5 5.5 %all-to-all-start = ((bf16[8,4,2,128,128]{4,3,2,1,0:T(8,128)(2,1)}), bf16[8,4,2,128,128]{4,3,2,1,0:T(8,128)(2,1)}, u32[]{:S(2)}, u32[]{:S(2)}) async-start(bf16[8,4,2,128,128]{4,3,2,1,0:T(8,128)(2,1)} %get-tuple-element.6), calls=%async_computation | async-start | bytes 4194304 | tf_op jit(solution)/shard_map/all_to_all | solution.py:460
  147.0 0.0 copy-start.2
  147.0 8.3 %fusion.4.q_ref = f32[512,1024]{1,0:T(8,128)S(1)} fusion(bf16[1,4096,1024]{2,1,0:T(8,128)(2,1)} %param.16, bf16[1,512,4096]{2,1,0:T(8,128)(2,1)} %param.14, f32[4096]{0:T(1024)S(1)} %bitcast.41, f32[512]{0:T(512)S(1)} %add_rsqrt_fusion), kind=kOutput, calls=%fused_computation.5 | convolution fusion | flops 4303355904 | bytes 14698496 | tf_op jit(solution)/shard_map/dot_general | solution.py:464
  155.3 0.0 copy-done.2
  155.3 25.9 %attend_1.1.a1_ref = bf16[4,512,512]{2,1,0:T(8,128)(2,1)S(1)} custom-call(f32[512,1024]{1,0:T(8,128)S(1)} %fusion.4.q_ref, f32[512,1024]{1,0:T(8,128)} %fusion.2.k_ref, bf16[512,1024]{1,0:T(8,128)(2,1)S(1)} %copy-done.2, bf16[8,4,2,128,128]{4,3,2,1,0:T(8,128)(2,1)} %copy-done.6, f32[512,128]{1,0:T(8,128)S(1)} %get-tuple-element.10.cos_ref, ...), custom_call_target="tpu_custom_call" | custom-call | flops 6442450944 | bytes 8388608 | tf_op jit(solution)/shard_map/attend_1/pallas_call | solution.py:130
  181.2 0.0 copy-start
  181.2 1.4 copy-done
  182.6 0.0 all-to-all-done.kv_ref
  182.6 0.0 copy-start.3
  182.6 1.2 copy-done.3
  183.8 23.7 %attend_0.1.a0_ref = bf16[4,512,512]{2,1,0:T(8,128)(2,1)S(1)} custom-call(f32[512,1024]{1,0:T(8,128)S(1)} %fusion.4.q_ref, f32[512,1024]{1,0:T(8,128)} %fusion.2.k_ref, bf16[512,1024]{1,0:T(8,128)(2,1)S(1)} %copy-done.3, bf16[8,4,2,128,128]{4,3,2,1,0:T(8,128)(2,1)} %all-to-all-done.kv_ref, f32[512,128]{1,0:T(8,128)S(1)} %get-tuple-element.10.cos_ref, ...), custom_call_target="tpu_custom_call" | custom-call | flops 6442450944 | bytes 8388608 | tf_op jit(solution)/shard_map/attend_0/pallas_call | solution.py:130
  207.6 0.0 copy-start.1
  207.6 1.3 copy-done.1
  208.9 0.0 collective-permute-done.wo_ref
  208.9 154.8 %mlp.1 = bf16[512,4096]{1,0:T(8,128)(2,1)} custom-call(bf16[4,512,512]{2,1,0:T(8,128)(2,1)} %copy-done.1, bf16[4,512,512]{2,1,0:T(8,128)(2,1)} %copy-done, bf16[4,512,1024]{2,1,0:T(8,128)(2,1)} %all-to-all-done.2.wm_ref, bf16[4,512,1024]{2,1,0:T(8,128)(2,1)} %collective-permute-done.wo_ref, bf16[512,4096]{1,0:T(8,128)(2,1)} %bitcast.37, ...), custom_call_target="tpu_custom_call" | custom-call | flops 38923141120 | bytes 167772160 | tf_op jit(solution)/shard_map/mlp/pallas_call | solution.py:414
  363.7 4.7 %copy.24 = bf16[1,512,4096]{2,1,0:T(8,128)(2,1)} copy(bf16[1,512,4096]{2,1,0:T(8,128)(2,1)} %bitcast.38) | data formatting | bytes 8388608
  (5 shorter events, 0.0 us)
Async XLA Ops:
  17.5 6.6 %copy-start.7 = (bf16[1,4096]{1,0:T(2,128)(2,1)S(1)}, bf16[1,4096]{1,0:T(2,128)(2,1)}, u32[]{:S(2)}) copy-start(bf16[1,4096]{1,0:T(2,128)(2,1)} %param.15) | copy-start | bytes 24580
  17.5 6.6 %copy-start.8 = (s32[8,1,1]{0,2,1:T(1,128)S(1)}, s32[8,1,1]{0,2,1:T(1,128)}, u32[]{:S(2)}) copy-start(s32[8,1,1]{0,2,1:T(1,128)} %param.13) | copy-start | bytes 100
  17.5 91.3 %all-to-all-start.2 = ((bf16[4,512,1024]{2,1,0:T(8,128)(2,1)}), bf16[4,512,1024]{2,1,0:T(8,128)(2,1)}, u32[]{:S(2)}, u32[]{:S(2)}) async-start(bf16[4,512,1024]{2,1,0:T(8,128)(2,1)} %bitcast.34), calls=%async_computation.2 | async-start | bytes 8388608 | tf_op jit(solution)/shard_map/all_to_all | solution.py:461
  93.4 3.4 copy-start.4
  96.8 3.7 %copy-start.5 = (bf16[1,512,4096]{2,1,0:T(8,128)(2,1)S(1)}, bf16[1,512,4096]{2,1,0:T(8,128)(2,1)}, u32[]{:S(2)}) copy-start(bf16[1,512,4096]{2,1,0:T(8,128)(2,1)} %param.14) | copy-start | bytes 12582916
  108.7 31.5 %all-to-all-start.1 = ((bf16[8,4,2,128,128]{4,3,2,1,0:T(8,128)(2,1)}), bf16[8,4,2,128,128]{4,3,2,1,0:T(8,128)(2,1)S(1)}, u32[]{:S(2)}, u32[]{:S(2)}) async-start(bf16[8,4,2,128,128]{4,3,2,1,0:T(8,128)(2,1)} %get-tuple-element.5), calls=%async_computation.1 | async-start | bytes 4194304 | tf_op jit(solution)/shard_map/all_to_all | solution.py:460
  115.4 93.5 %collective-permute-start = (bf16[4,512,1024]{2,1,0:T(8,128)(2,1)}, bf16[4,512,1024]{2,1,0:T(8,128)(2,1)}, u32[]{:S(2)}, u32[]{:S(2)}) collective-permute-start(bf16[4,512,1024]{2,1,0:T(8,128)(2,1)} %all-to-all-done.2.wm_ref), channel_id=1, source_target_pairs={{0,1},{1,0},{2,3},{3,2},{4,5},{5,4},{6,7},{7,6},{8,9},{9,8},{10,11... | collective-permute-start | bytes 12582920 | tf_op jit(solution)/shard_map/ppermute | solution.py:462
  140.2 1.4 copy-start.6
  141.5 41.0 %all-to-all-start = ((bf16[8,4,2,128,128]{4,3,2,1,0:T(8,128)(2,1)}), bf16[8,4,2,128,128]{4,3,2,1,0:T(8,128)(2,1)}, u32[]{:S(2)}, u32[]{:S(2)}) async-start(bf16[8,4,2,128,128]{4,3,2,1,0:T(8,128)(2,1)} %get-tuple-element.6), calls=%async_computation | async-start | bytes 4194304 | tf_op jit(solution)/shard_map/all_to_all | solution.py:460
  147.0 8.3 %copy-start.2 = (bf16[512,1024]{1,0:T(8,128)(2,1)S(1)}, bf16[512,1024]{1,0:T(8,128)(2,1)}, u32[]{:S(2)}) copy-start(bf16[512,1024]{1,0:T(8,128)(2,1)} %fusion.7.v_ref) | copy-start | bytes 3145732
  181.2 1.4 copy-start
  182.6 1.2 copy-start.3
  207.6 1.3 copy-start.1

commit v2 on v0

v2 whole, which is shorter than its diff:
```python
import functools

import jax
import jax.numpy as jnp
from jax import lax
from jax.experimental import pallas as pl
from jax.experimental.pallas import tpu as pltpu
from jax.sharding import PartitionSpec as P

MESH = pl.DeviceIdType.MESH
BF16 = jnp.bfloat16
F32 = jnp.float32
ANY = pl.BlockSpec(memory_space=pl.ANY)
VMEM_MAX = 67043328


def rope_tables(prefix, tokens, head_dim):
    positions = (prefix + jnp.arange(tokens)).astype(F32)
    inv_freq = 10000.0 ** (-2.0 * jnp.arange(head_dim // 2).astype(F32) / head_dim)
    angles = positions[:, None] * inv_freq[None, :]
    cos_half, sin_half = jnp.cos(angles), jnp.sin(angles)
    return jnp.concatenate([cos_half, cos_half], axis=-1), jnp.concatenate([-sin_half, sin_half], axis=-1)


NT = (((1,), (1,)), ((), ()))


def remote(src, dst, send_sem, recv_sem, **target):
    return pltpu.make_async_remote_copy(
        src_ref=src, dst_ref=dst, send_sem=send_sem, recv_sem=recv_sem, device_id=target, device_id_type=MESH
    )


def signal_all(targets):
    barrier = pltpu.get_barrier_semaphore()
    for target in targets:
        pl.semaphore_signal(barrier, inc=1, device_id=target, device_id_type=MESH)
    pl.semaphore_wait(barrier, len(targets))


PAIR = 256


def front_kernel(ring, owners, kv_ref, x_ref, wq_ref, wk_ref, wv_ref, wo_ref, gain_ref, cos_ref, sin_ref, mid_ref,
                 x_buf, normed, w_buf, proj, kv_buf, gathered, wo_buf, own_wo, total, mid_buf,
                 local_sem, w_sem, kv_send, kv_recv, a_send, a_recv, wo_send, wo_recv):
    me, here = lax.axis_index("heads"), lax.axis_index("pool")
    right, left = lax.rem(me + 1, ring), lax.rem(me + ring - 1, ring)
    tokens, width = x_ref.shape
    heads = kv_buf.shape[1]
    head_dim = kv_buf.shape[-1]
    prefix = owners * kv_buf.shape[2] * kv_buf.shape[4]
    block = width // ring
    half = tokens // 2
    scale = head_dim ** -0.5
    pairs = heads * head_dim // PAIR
    per_pair = PAIR // head_dim
    w_refs = (wq_ref, wk_ref, wv_ref)

    def load_pair(hp):
        cols = pl.ds(pl.multiple_of(hp * PAIR, PAIR), PAIR)
        slot = lax.rem(hp, 2)
        return [pltpu.make_async_copy(w_refs[m].at[:, cols], w_buf.at[slot, m], w_sem.at[slot, m]) for m in range(3)]

    x_copy = pltpu.make_async_copy(x_ref, x_buf, local_sem.at[0])
    x_copy.start()
    kv_own = pltpu.make_async_copy(kv_ref.at[here], kv_buf.at[here], local_sem.at[1])
    kv_own.start()
    for copy in load_pair(0):
        copy.start()
    wo_own = pltpu.make_async_copy(wo_ref.at[:, pl.ds(pl.multiple_of(me * block, block), block)], own_wo, local_sem.at[2])
    wo_own.start()

    signal_all([{"pool": lax.rem(here + t, owners)} for t in range(1, owners)] + [{"heads": lax.rem(me + u, ring)} for u in range(1, ring)])

    piece_rows = wo_ref.shape[0] // owners

    def wo_bring(u):
        dest = lax.rem(me + u, ring)
        src = wo_ref.at[pl.ds(pl.multiple_of(here * piece_rows, piece_rows), piece_rows), pl.ds(pl.multiple_of(dest * block, block), block)]
        return remote(src, wo_buf.at[u - 1, here], wo_send.at[u - 1], wo_recv.at[u - 1], heads=dest)

    chip_right, chip_left = lax.rem(here + 2, owners), lax.rem(here + owners - 2, owners)
    partner = here + 1 - 2 * lax.rem(here, 2)
    across = lax.rem(here + owners // 2, owners)
    half_rows = piece_rows // 2

    def wo_spread(i):
        piece = wo_buf.at[:, here]
        return remote(piece, piece, wo_send.at[3 + i], wo_recv.at[3 + i], pool=(chip_right, chip_left, partner)[i])

    def wo_onward(i):
        piece = wo_buf.at[:, (chip_left, chip_right)[i], pl.ds(i * half_rows, half_rows)]
        return remote(piece, piece, wo_send.at[6 + i], wo_recv.at[6 + i], pool=(chip_right, chip_left)[i])

    def wo_beside(i):
        piece = wo_buf.at[:, (chip_left, chip_right)[i]]
        return remote(piece, piece, wo_send.at[8 + i], wo_recv.at[8 + i], pool=partner)

    def wo_beside_far(i):
        piece = wo_buf.at[:, across, pl.ds(i * half_rows, half_rows)]
        return remote(piece, piece, wo_send.at[10 + i], wo_recv.at[10 + i], pool=partner)

    for u in range(1, ring):
        wo_bring(u).start()

    def page_copy(g, t):
        dest = lax.rem(here + t, owners)
        return remote(kv_ref.at[dest, g], kv_buf.at[here, g], kv_send.at[t - 1, g], kv_recv.at[t - 1, g], pool=dest)

    order = sorted(range(1, owners), key=lambda t: -min(t, owners - t))

    def send_pages(g, carry):
        for t in order:
            page_copy(g, t).start()
        return carry

    lax.fori_loop(0, heads, send_pages, 0)

    x_copy.wait()
    step = 64

    def normalise(i, carry):
        rows = pl.ds(pl.multiple_of(i * step, step), step)
        val = x_buf[rows].astype(F32)
        inv_rms = lax.rsqrt(jnp.mean(val * val, axis=-1, keepdims=True) + 1e-5)
        normed[rows] = (val * inv_rms * gain_ref[...].astype(F32)).astype(BF16)
        return carry

    lax.fori_loop(0, tokens // step, normalise, 0)
    kv_own.wait()

    def lanes(g):
        return pl.ds(pl.multiple_of(g * head_dim, head_dim), head_dim)

    def a_direct(g, way):
        piece = gathered.at[me, :, lanes(g)]
        return remote(piece, piece, a_send.at[g, 0, way], a_recv.at[g, 0, way], heads=(right, left)[way])

    def a_passed(g, way):
        piece = gathered.at[(left, right)[way], pl.ds(way * half, half), lanes(g)]
        return remote(piece, piece, a_send.at[g, 1, way], a_recv.at[g, 1, way], heads=(right, left)[way])

    def a_forward(g):
        for way in range(2):
            a_direct(g, way).wait_recv()
            a_passed(g, way).start()

    def rope(val):
        return (val * cos_ref[...] + pltpu.roll(val, head_dim // 2, 1) * sin_ref[...]).astype(BF16)

    def attend(hp, sub):
        g = hp * per_pair + sub
        cols = slice(sub * head_dim, (sub + 1) * head_dim)
        for t in range(1, owners):
            page_copy(g, t).wait_recv()
        keys_pre = kv_buf[:, g, :, 0].reshape(prefix, head_dim)
        vals_pre = kv_buf[:, g, :, 1].reshape(prefix, head_dim)
        for part in range(2):
            rows = slice(part * half, (part + 1) * half)
            seen = (part + 1) * half
            q_part = proj[0, rows, cols]
            s_pre = lax.dot_general(q_part, keys_pre, NT, preferred_element_type=F32) * scale
            s_new = lax.dot_general(q_part, proj[1, :seen, cols], NT, preferred_element_type=F32) * scale
            t_id = lax.broadcasted_iota(jnp.int32, s_new.shape, 0) + part * half
            u_id = lax.broadcasted_iota(jnp.int32, s_new.shape, 1)
            s_new = jnp.where(t_id >= u_id, s_new, -jnp.inf)
            row_max = jnp.maximum(jnp.max(s_pre, axis=-1, keepdims=True), jnp.max(s_new, axis=-1, keepdims=True))
            e_pre = jnp.exp(s_pre - row_max)
            e_new = jnp.exp(s_new - row_max)
            inv_den = 1.0 / (jnp.sum(e_pre, axis=-1, keepdims=True) + jnp.sum(e_new, axis=-1, keepdims=True))
            out = jnp.dot((e_pre * inv_den).astype(BF16), vals_pre, preferred_element_type=F32)
            out = out + jnp.dot((e_new * inv_den).astype(BF16), proj[2, :seen, cols], preferred_element_type=F32)
            gathered[me, rows, lanes(g)] = out.astype(BF16)
        for way in range(2):
            a_direct(g, way).start()

    def one_pair(hp, carry):
        for copy in load_pair(hp):
            copy.wait()

        @pl.when(hp + 1 < pairs)
        def _():
            for copy in load_pair(hp + 1):
                copy.start()

        slot = lax.rem(hp, 2)
        for m in range(3):
            val = jnp.dot(normed[...], w_buf[slot, m], preferred_element_type=F32)
            for sub in range(per_pair):
                cols = slice(sub * head_dim, (sub + 1) * head_dim)
                proj[m, :, cols] = rope(val[:, cols]) if m < 2 else val[:, cols].astype(BF16)
        for sub in range(per_pair):
            attend(hp, sub)
            g = hp * per_pair + sub

            @pl.when(g > 0)
            def _():
                a_forward(g - 1)

        @pl.when(hp == pairs // 2)
        def _():
            for u in range(1, ring):
                wo_bring(u).wait_recv()
            for i in range(3):
                wo_spread(i).start()

        return carry

    lax.fori_loop(0, pairs, one_pair, 0)
    a_forward(heads - 1)
    wo_own.wait()
    total[...] = jnp.dot(gathered[me], own_wo[...], preferred_element_type=F32)

    for i in range(2):
        wo_spread(i).wait_recv()
        wo_onward(i).start()
        wo_beside(i).start()

    def a_settle(g, carry):
        for way in range(2):
            a_direct(g, way).wait_send()
            a_passed(g, way).wait()
        return carry

    lax.fori_loop(0, heads, a_settle, 0)
    for i in range(2):
        wo_onward(i).wait_recv()
        wo_beside_far(i).start()
    wo_spread(2).wait_recv()
    for i in range(2):
        wo_beside(i).wait_recv()
    for i in range(2):
        wo_beside_far(i).wait_recv()

    for n in range(2):
        cols = slice(n * block // 2, (n + 1) * block // 2)
        res = total[:, cols]
        for u in range(1, ring):
            weight = wo_buf[u - 1, :, :, cols].reshape(owners * piece_rows, block // 2)
            res = res + jnp.dot(gathered[lax.rem(me + ring - u, ring)], weight, preferred_element_type=F32)
        x_cols = pl.ds(pl.multiple_of(me * block + n * (block // 2), block // 2), block // 2)
        mid_buf[:, cols] = (x_buf[:, x_cols].astype(F32) + res).astype(BF16)
    mid_copy = pltpu.make_async_copy(mid_buf, mid_ref, local_sem.at[0])
    mid_copy.start()

    def page_settle(g, carry):
        for t in range(1, owners):
            page_copy(g, t).wait_send()
        return carry

    lax.fori_loop(0, heads, page_settle, 0)
    for u in range(1, ring):
        wo_bring(u).wait_send()
    for i in range(3):
        wo_spread(i).wait_send()
    for i in range(2):
        wo_onward(i).wait_send()
        wo_beside(i).wait_send()
        wo_beside_far(i).wait_send()
    mid_copy.wait()


def front(call_id, ring, owners, kv, x, w_q, w_k, w_v, w_o, gain, cos_tab, sin_tab):
    tokens, width = x.shape
    heads, head_dim = kv.shape[1], kv.shape[-1]
    block = width // ring
    local = heads * head_dim
    dma = pltpu.SemaphoreType.DMA
    in_vmem = pl.BlockSpec(memory_space=pltpu.VMEM)
    return pl.pallas_call(
        functools.partial(front_kernel, ring, owners),
        out_shape=jax.ShapeDtypeStruct((tokens, block), BF16),
        in_specs=[ANY] * 6 + [in_vmem] * 3,
        out_specs=ANY,
        scratch_shapes=[
            pltpu.VMEM((tokens, width), BF16),
            pltpu.VMEM((tokens, width), BF16),
            pltpu.VMEM((2, 3, width, PAIR), BF16),
            pltpu.VMEM((3, tokens, PAIR), BF16),
            pltpu.VMEM(kv.shape, BF16),
            pltpu.VMEM((ring, tokens, local), BF16),
            pltpu.VMEM((ring - 1, owners, local // owners, block), BF16),
            pltpu.VMEM((local, block), BF16),
            pltpu.VMEM((tokens, block), F32),
            pltpu.VMEM((tokens, block), BF16),
            dma((3,)), dma((2, 3)),
            dma((owners - 1, heads)), dma((owners - 1, heads)),
            dma((heads, 2, 2)), dma((heads, 2, 2)),
            dma((12,)), dma((12,)),
        ],
        compiler_params=pltpu.CompilerParams(collective_id=call_id, has_side_effects=True, vmem_limit_bytes=VMEM_MAX),
        cost_estimate=pl.CostEstimate(flops=8 * tokens * width * local, bytes_accessed=48 * 2**20, transcendentals=heads * tokens * 3 * tokens),
        name="front",
    )(kv, x, w_q, w_k, w_v, w_o, gain, cos_tab, sin_tab)


CHUNKS = 2
GROUPS = 4
N_BLOCK = 256


def mlp_kernel(ring, x_ref, gain_ref, wg_ref, wu_ref, wd_ref, out_ref,
               mid, normed, gate_w, up_w, act, down_w, part_sum, running, result,
               local_sem, w_sem, d_sem, mid_send, mid_recv, rs_send, rs_recv, ag_send, ag_recv, out_sem):
    me = lax.axis_index("heads")
    right, left = lax.rem(me + 1, ring), lax.rem(me + ring - 1, ring)
    ways = (right, left)
    tokens, block = x_ref.shape
    width = block * ring
    hid = wg_ref.shape[0]
    rows_c = tokens // CHUNKS
    rows_g = tokens // GROUPS
    per_chunk = GROUPS // CHUNKS
    n_half = block // 2
    n_full, n_rest = hid // N_BLOCK, hid % N_BLOCK
    n_steps = n_full + 1

    x_copies = []
    for c in range(CHUNKS):
        rows = pl.ds(c * rows_c, rows_c)
        x_copies.append(pltpu.make_async_copy(x_ref.at[rows], mid.at[me, rows], local_sem.at[c]))
        x_copies[c].start()

    def load_full(c, i):
        rows = pl.ds(pl.multiple_of(i * N_BLOCK, N_BLOCK), N_BLOCK)
        slot = lax.rem(c * n_steps + i, 3)
        return (pltpu.make_async_copy(wg_ref.at[rows], gate_w.at[slot], w_sem.at[0, slot]),
                pltpu.make_async_copy(wu_ref.at[rows], up_w.at[slot], w_sem.at[1, slot]))

    def load_rest(c):
        rows, dst = pl.ds(n_full * N_BLOCK, n_rest), pl.ds(0, n_rest)
        slot = (c * n_steps + n_full) % 3
        return (pltpu.make_async_copy(wg_ref.at[rows], gate_w.at[slot, dst], w_sem.at[0, slot]),
                pltpu.make_async_copy(wu_ref.at[rows], up_w.at[slot, dst], w_sem.at[1, slot]))

    def run(copies):
        for copy in copies:
            copy.start()

    def load_down(jj):
        s, way = lax.rem(jj // 2, ring), lax.rem(jj, 2)
        blk = jnp.where(way == 0, lax.rem(me + 2 * ring - 1 - s, ring), lax.rem(me + 1 + s, ring))
        col = pl.multiple_of(blk * block + way * n_half, n_half)
        slot = lax.rem(jj, 3)
        return pltpu.make_async_copy(wd_ref.at[:, pl.ds(col, n_half)], down_w.at[slot], d_sem.at[slot])

    run(load_full(0, 0))
    run(load_full(0, 1))
    for jj in range(2):
        load_down(jj).start()

    signal_all([{"heads": right}, {"heads": left}])

    def mid_direct(c, way):
        piece = mid.at[me, pl.ds(c * rows_c, rows_c)]
        return remote(piece, piece, mid_send.at[c, 0, way], mid_recv.at[c, 0, way], heads=ways[way])

    def mid_passed(c, way):
        piece = mid.at[(left, right)[way], pl.ds(c * rows_c + way * (rows_c // 2), rows_c // 2)]
        return remote(piece, piece, mid_send.at[c, 1, way], mid_recv.at[c, 1, way], heads=ways[way])

    def mid_start(c):
        x_copies[c].wait()
        for way in range(2):
            mid_direct(c, way).start()

    def mid_forward(c):
        for way in range(2):
            mid_direct(c, way).wait_recv()
            mid_passed(c, way).start()

    def mid_settle(c):
        for way in range(2):
            mid_passed(c, way).wait_recv()

    def rs_send_copy(r, s, way):
        rows = pl.ds((r % per_chunk) * rows_g, rows_g)
        src = part_sum.at[r // per_chunk, 0, way, rows] if s == 0 else running.at[r, s - 1, way]
        return remote(src, running.at[r, s, way], rs_send.at[r, s, way], rs_recv.at[r, s, way], heads=ways[way])

    def rs_step(r, s):
        rows = slice((r % per_chunk) * rows_g, (r % per_chunk + 1) * rows_g)
        for way in range(2):
            rs_send_copy(r, s - 1, way).wait_recv()
            running[r, s - 1, way] = running[r, s - 1, way] + part_sum[r // per_chunk, s, way, rows]
            rs_send_copy(r, s, way).start()

    def ag_direct(r, way):
        piece = result.at[me, pl.ds(r * rows_g, rows_g)]
        return remote(piece, piece, ag_send.at[r, 0, way], ag_recv.at[r, 0, way], heads=ways[way])

    def ag_passed(r, way):
        piece = result.at[(left, right)[way], pl.ds(r * rows_g + way * (rows_g // 2), rows_g // 2)]
        return remote(piece, piece, ag_send.at[r, 1, way], ag_recv.at[r, 1, way], heads=ways[way])

    def rs_final(r):
        rows = slice((r % per_chunk) * rows_g, (r % per_chunk + 1) * rows_g)
        dst = slice(r * rows_g, (r + 1) * rows_g)
        for way in range(2):
            rs_send_copy(r, ring - 2, way).wait_recv()
            cols = slice(way * n_half, (way + 1) * n_half)
            total = running[r, ring - 2, way] + part_sum[r // per_chunk, ring - 1, way, rows]
            result[me, dst, cols] = (mid[me, dst, cols].astype(F32) + total).astype(BF16)
        for way in range(2):
            ag_direct(r, way).start()

    def ag_forward(r):
        for way in range(2):
            ag_direct(r, way).wait_recv()
            ag_passed(r, way).start()

    def put_out(r, src):
        rows = pl.ds(r * rows_g, rows_g)
        return pltpu.make_async_copy(result.at[src, rows], out_ref.at[rows, pl.ds(src * block, block)], out_sem.at[r, src])

    def ag_settle(r):
        for way in range(2):
            ag_passed(r, way).wait_recv()
        for src in range(ring):
            put_out(r, src).start()

    def normalise(c):
        step = 64

        def body(i, carry):
            base = pl.multiple_of(i * step, step)
            rows, out_rows = pl.ds(c * rows_c + base, step), pl.ds(base, step)
            squares = jnp.zeros((step, 1), F32)
            for b in range(ring):
                val = mid[b, rows].astype(F32)
                squares = squares + jnp.sum(val * val, axis=-1, keepdims=True)
            inv_rms = lax.rsqrt(squares * (1.0 / width) + 1e-5)
            for b in range(ring):
                cols = slice(b * block, (b + 1) * block)
                normed[out_rows, cols] = (mid[b, rows].astype(F32) * inv_rms * gain_ref[:, cols].astype(F32)).astype(BF16)
            return carry

        lax.fori_loop(0, rows_c // step, body, 0)

    def hidden_block(gate_rows, up_rows):
        gate = lax.dot_general(normed[...], gate_rows, NT, preferred_element_type=F32)
        up = lax.dot_general(normed[...], up_rows, NT, preferred_element_type=F32)
        return (gate * jax.nn.sigmoid(gate) * up).astype(BF16)

    def gate_up(c, tasks):
        def body(i, carry):
            slot = lax.rem(c * n_steps + i, 3)
            for copy in load_full(c, i):
                copy.wait()
            pl.when(i + 2 < n_full)(lambda: run(load_full(c, i + 2)))
            pl.when(i + 2 == n_full)(lambda: run(load_rest(c)))
            if c + 1 < CHUNKS:
                pl.when(i + 2 == n_full + 1)(lambda: run(load_full(c + 1, 0)))
            act[:, pl.ds(pl.multiple_of(i * N_BLOCK, N_BLOCK), N_BLOCK)] = hidden_block(gate_w[slot], up_w[slot])
            for at, task in tasks:
                pl.when(i == at)(task)
            return carry

        lax.fori_loop(0, n_full, body, 0)
        for copy in load_rest(c):
            copy.wait()
        if c + 1 < CHUNKS:
            run(load_full(c + 1, 1))
        slot = (c * n_steps + n_full) % 3
        act[:, n_full * N_BLOCK:] = hidden_block(gate_w[slot, :n_rest], up_w[slot, :n_rest])

    def down(c, tasks):
        def body(s, carry):
            for way in range(2):
                jj = c * 2 * ring + 2 * s + way
                load_down(jj).wait()
                pl.when(jj + 2 < CHUNKS * 2 * ring)(lambda: load_down(jj + 2).start())
                part_sum[c, s, way] = jnp.dot(act[...], down_w[lax.rem(jj, 3)], preferred_element_type=F32)

            @pl.when(s == 0)
            def _():
                for sub in range(per_chunk):
                    for way in range(2):
                        rs_send_copy(c * per_chunk + sub, 0, way).start()

            for at, task in tasks:
                pl.when(s == at)(task)
            return carry

        lax.fori_loop(0, ring, body, 0)

    do = functools.partial
    mid_start(0)
    mid_forward(0)
    mid_start(1)
    mid_settle(0)
    normalise(0)
    gate_up(0, [(7, do(mid_forward, 1))])
    down(0, [])
    mid_settle(1)
    normalise(1)
    gate_up(1, [(2, do(rs_step, 0, 1)), (5, do(rs_step, 1, 1)), (8, do(rs_step, 0, 2))])
    down(1, [(0, do(rs_step, 1, 2)), (2, do(rs_final, 0)), (3, do(rs_final, 1))])
    rs_step(2, 1)
    rs_step(3, 1)
    ag_forward(0)
    ag_forward(1)
    rs_step(2, 2)
    rs_step(3, 2)
    ag_settle(0)
    ag_settle(1)
    rs_final(2)
    rs_final(3)
    ag_forward(2)
    ag_forward(3)
    ag_settle(2)
    ag_settle(3)
    for c in range(CHUNKS):
        for way in range(2):
            mid_direct(c, way).wait_send()
            mid_passed(c, way).wait_send()
    for r in range(GROUPS):
        for way in range(2):
            for s in range(ring - 1):
                rs_send_copy(r, s, way).wait_send()
            ag_direct(r, way).wait_send()
            ag_passed(r, way).wait_send()
        for src in range(ring):
            put_out(r, src).wait()


def mlp(call_id, ring, x_mid, gain, w_gate, w_up, w_down):
    tokens, block = x_mid.shape
    hid, width = w_gate.shape
    rows_c, rows_g = tokens // CHUNKS, tokens // GROUPS
    dma = pltpu.SemaphoreType.DMA
    return pl.pallas_call(
        functools.partial(mlp_kernel, ring),
        out_shape=jax.ShapeDtypeStruct((tokens, width), BF16),
        in_specs=[ANY, pl.BlockSpec(memory_space=pltpu.VMEM), ANY, ANY, ANY],
        out_specs=ANY,
        scratch_shapes=[
            pltpu.VMEM((ring, tokens, block), BF16),
            pltpu.VMEM((rows_c, width), BF16),
            pltpu.VMEM((3, N_BLOCK, width), BF16),
            pltpu.VMEM((3, N_BLOCK, width), BF16),
            pltpu.VMEM((rows_c, hid), BF16),
            pltpu.VMEM((3, hid, block // 2), BF16),
            pltpu.VMEM((CHUNKS, ring, 2, rows_c, block // 2), F32),
            pltpu.VMEM((GROUPS, ring - 1, 2, rows_g, block // 2), F32),
            pltpu.VMEM((ring, tokens, block), BF16),
            dma((CHUNKS,)), dma((2, 3)), dma((3,)),
            dma((CHUNKS, 2, 2)), dma((CHUNKS, 2, 2)),
            dma((GROUPS, ring - 1, 2)), dma((GROUPS, ring - 1, 2)),
            dma((GROUPS, 2, 2)), dma((GROUPS, 2, 2)),
            dma((GROUPS, ring)),
        ],
        compiler_params=pltpu.CompilerParams(collective_id=call_id, has_side_effects=True, vmem_limit_bytes=VMEM_MAX),
        cost_estimate=pl.CostEstimate(flops=6 * tokens * width * hid, bytes_accessed=140 * 2**20, transcendentals=tokens * hid),
        name="mlp",
    )(x_mid, gain, w_gate, w_up, w_down)


def solution(mesh):
    owners = mesh.shape["pool"]
    ring = mesh.shape["heads"]
    assert ring == 4 and owners == 8

    def local_fn(kv_pool, page_idx, x_tokens, gain_attn, w_q, w_k, w_v, w_o, gain_mlp, w_gate, w_up, w_down):
        layers, _, _, page_len, kv_loc, head_dim = kv_pool.shape
        tokens = x_tokens.shape[1]
        req_pages = page_idx.shape[2]
        wanted = page_idx.reshape(owners * req_pages)
        cos_tab, sin_tab = rope_tables(owners * req_pages * page_len, tokens, head_dim)
        hidden = x_tokens[0]
        for layer in range(layers):
            picked = kv_pool.at[layer, wanted].get(mode="promise_in_bounds")
            picked = picked.reshape(owners, req_pages, 2, page_len, kv_loc, head_dim).transpose(0, 4, 1, 2, 3, 5)
            x_mid = front(2 * layer, ring, owners, picked, hidden, w_q[layer], w_k[layer], w_v[layer], w_o[layer], gain_attn[layer][None], cos_tab, sin_tab)
            hidden = mlp(2 * layer + 1, ring, x_mid, gain_mlp[layer][None], w_gate[layer].T, w_up[layer].T, w_down[layer])
        return hidden[None]

    pool_spec = P(None, ("rep", "pool"), None, None, "heads", None)
    index_spec = P("rep", "pool", None)
    x_spec = P(("rep", "pool"), None, None)
    gain_spec = P(None, None)
    col_spec = P(None, None, "heads")
    row_spec = P(None, "heads", None)
    return jax.shard_map(local_fn, mesh=mesh, in_specs=(pool_spec, index_spec, x_spec, gain_spec, col_spec, col_spec, col_spec, row_spec, gain_spec, col_spec, col_spec, row_spec), out_specs=x_spec, check_vma=False)
```

time: 522 us -> 258 us (0.49); the launches traced: 515 us -> 258 us
  waiting for transfers between devices: 311 us -> 0 us
  Pallas kernels: 0 us -> 238 us
  matrix products: 114 us -> 0 us
  other arithmetic: 35.2 us -> 2.67 us
  local copies, waits for them, and re-layouts: 33.5 us -> 16.5 us
  between operations: 14.1 us -> 0.03 us
  starting transfers between devices: 6.57 us -> 0 us
    psum x2 -> x0, waiting for transfers between devices: 311 us -> none  [the longest x1 156 us: local_fn(): lax.psum(jnp.dot(attn_cat, w_o[layer_id], preferred_element_type=jnp.floa...]
    pallas_call x0 -> x2, Pallas kernels: none -> 238 us  [the longest x1 149 us: mlp(): pl.pallas_call(functools.partial(mlp_kernel, ring), out_shape=jax.ShapeDt...]
    dot_general x11 -> x0, matrix products: 114 us -> none  [the longest x1 19.7 us: local_fn(): jnp.dot(h_mlp, w_gate[layer_id], preferred_element_type=jnp.float32)]
    dot_general x2 -> x0, local copies, waits for them, and re-layouts: 22.8 us -> none  [the longest x1 11.5 us: local_fn(): jnp.dot(h_att, w_k[layer_id], preferred_element_type=jnp.float32)]
    reduce_sum x4 -> x0, other arithmetic: 19.8 us -> none  [the longest x2 9.37 us: rms_norm(): jnp.mean(hid_f32 * hid_f32, axis=-1, keepdims=True) + 1e-05]
    broadcast_in_dim x1 -> x0, other arithmetic: 8 us -> none  [local_fn(): return hidden[None]]
    all_to_all x1 -> x0, starting transfers between devices: 6.5 us -> none  [local_fn(): received = lax.all_to_all(picked, 'pool', 0, 0, tiled=True)]
    select_n x2 -> x0, other arithmetic: 5.33 us -> none  [local_fn(): picked = jnp.take(kv_pool[layer_id], wanted, axis=0)]
  transfers between devices with their start and end apart: 3 -> 0, of which waited for: 2 -> 0; matrix products, arithmetic and copies ran while one was open for 11% -> 0% of each run, Pallas kernels for 0% -> 0%
where the time goes in v2:
time: 258 us
  Pallas kernels  238 us (92%)
  local copies, waits for them, and re-layouts  16.5 us (6%)
  other arithmetic  2.67 us (1%)
    pallas_call x1, Pallas kernels, mlp(): pl.pallas_call(functools.partial(mlp_kernel, ring), out_shape=jax.ShapeDt...  149 us
    pallas_call x1, Pallas kernels, front(): pl.pallas_call(functools.partial(front_kernel, ring, owners), out_shape=j...  89.5 us
    gather x2, local copies, waits for them, and re-layouts, local_fn(): picked = kv_pool.at[layer, wanted].get(mode='promise_in_bounds')  11.8 us

profile of v2, /device:TPU:97, one launch (start us, length us, event | category | flops | bytes accessed | tf_op | source)
XLA Modules:
  0.0 257.5 jit_solution(9598878885972478664)
XLA Ops:
  0.0 0.7 fusion.3
  0.7 6.5 %gather_fusion = bf16[8,2,128,8,128]{4,3,2,1,0:T(8,128)(2,1)} fusion(bf16[1,16,2,128,8,128]{5,4,3,2,1,0:T(8,128)(2,1)} %param.12, s32[8]{0:T(128)S(1)} %fusion.3), kind=kCustom, calls=%fused_computation | custom fusion | bytes 8388672 | tf_op jit(solution)/shard_map/gather | solution.py:573
  7.2 5.3 %copy.15 = bf16[8,2,128,8,128]{4,2,1,3,0:T(8,128)(2,1)} copy(bf16[8,2,128,8,128]{4,3,2,1,0:T(8,128)(2,1)} %gather_fusion) | data formatting | bytes 8388608 | tf_op jit(solution)/shard_map/gather | solution.py:573
  12.5 1.0 fusion
  13.5 1.0 pad_maximum_fusion
  14.5 89.5 %front.1.x_ref = bf16[512,1024]{1,0:T(8,128)(2,1)} custom-call(bf16[8,8,1,2,128,128]{5,4,3,2,1,0:T(8,128)(2,1)} %bitcast.22, bf16[512,4096]{1,0:T(8,128)(2,1)} %bitcast.31, bf16[4096,1024]{1,0:T(8,128)(2,1)} %bitcast.27, bf16[4096,1024]{1,0:T(8,128)(2,1)} %bitcast.28, bf16[4096,1024]{1,0:T(8,128)(2,1)} %bitcast.29, bf16[1024,4096]{1,0:T(8,128)(2,1)} %bitcast.30, ...), custom_call_target="tpu_custom_call" | custom-call | flops 17179869184 | bytes 50331648 | tf_op jit(solution)/shard_map/front/pallas_call | solution.py:271
  103.9 148.9 %mlp.1 = bf16[512,4096]{1,0:T(8,128)(2,1)} custom-call(bf16[512,1024]{1,0:T(8,128)(2,1)} %front.1.x_ref, bf16[1,4096]{1,0:T(2,128)(2,1)} %gain_ref.3, bf16[2752,4096]{1,0:T(8,128)(2,1)} %bitcast.24, bf16[2752,4096]{1,0:T(8,128)(2,1)} %bitcast.25, bf16[2752,4096]{1,0:T(8,128)(2,1)} %bitcast.26), custom_call_target="tpu_custom_call" | custom-call | flops 34628173824 | bytes 146800640 | tf_op jit(solution)/shard_map/mlp/pallas_call | solution.py:533
  252.8 4.7 %copy.17 = bf16[1,512,4096]{2,1,0:T(8,128)(2,1)} copy(bf16[1,512,4096]{2,1,0:T(8,128)(2,1)} %bitcast.23) | data formatting | bytes 8388608
  (2 shorter events, 0.0 us)

commit v3 on v2

--- a/solution.py
+++ b/solution.py
@@ -2,6 +2,7 @@
 
 import jax
 import jax.numpy as jnp
+import numpy as np
 from jax import lax
 from jax.experimental import pallas as pl
 from jax.experimental.pallas import tpu as pltpu
@@ -15,11 +16,32 @@
 
 
 def rope_tables(prefix, tokens, head_dim):
-    positions = (prefix + jnp.arange(tokens)).astype(F32)
-    inv_freq = 10000.0 ** (-2.0 * jnp.arange(head_dim // 2).astype(F32) / head_dim)
+    positions = (prefix + np.arange(tokens)).astype(np.float32)
+    inv_freq = np.float32(10000.0) ** (-2.0 * np.arange(head_dim // 2).astype(np.float32) / head_dim).astype(np.float32)
     angles = positions[:, None] * inv_freq[None, :]
-    cos_half, sin_half = jnp.cos(angles), jnp.sin(angles)
-    return jnp.concatenate([cos_half, cos_half], axis=-1), jnp.concatenate([-sin_half, sin_half], axis=-1)
+    cos_half, sin_half = np.cos(angles), np.sin(angles)
+    return np.concatenate([cos_half, cos_half], axis=-1), np.concatenate([-sin_half, sin_half], axis=-1)
+
+
+def pick_kernel(idx_ref, page_ref, out_ref):
+    for side in range(2):
+        out_ref[0, :, 0, side] = jnp.swapaxes(page_ref[0, side], 0, 1)
+
+
+def pick_pages(pool, wanted, owners):
+    _, _, page_len, heads, head_dim = pool.shape
+    each = wanted.shape[0] // owners
+    return pl.pallas_call(
+        pick_kernel,
+        grid_spec=pltpu.PrefetchScalarGridSpec(
+            num_scalar_prefetch=1,
+            grid=(wanted.shape[0],),
+            in_specs=[pl.BlockSpec((1, 2, page_len, heads, head_dim), lambda i, idx: (idx[i], 0, 0, 0, 0))],
+            out_specs=pl.BlockSpec((1, heads, 1, 2, page_len, head_dim), lambda i, idx: (i // each, 0, i % each, 0, 0, 0)),
+        ),
+        out_shape=jax.ShapeDtypeStruct((owners, heads, each, 2, page_len, head_dim), pool.dtype),
+        name="pick_pages",
+    )(wanted, pool)
 
 
 NT = (((1,), (1,)), ((), ()))
@@ -39,11 +61,12 @@
 
 
 PAIR = 256
+SPREAD = 64
 
 
 def front_kernel(ring, owners, kv_ref, x_ref, wq_ref, wk_ref, wv_ref, wo_ref, gain_ref, cos_ref, sin_ref, mid_ref,
                  x_buf, normed, w_buf, proj, kv_buf, gathered, wo_buf, own_wo, total, mid_buf,
-                 local_sem, w_sem, kv_send, kv_recv, a_send, a_recv, wo_send, wo_recv):
+                 local_sem, w_sem, kv_send, kv_recv, a_send, a_recv, wo_send, wo_recv, rest_send, rest_recv):
     me, here = lax.axis_index("heads"), lax.axis_index("pool")
     right, left = lax.rem(me + 1, ring), lax.rem(me + ring - 1, ring)
     tokens, width = x_ref.shape
@@ -74,35 +97,58 @@
     signal_all([{"pool": lax.rem(here + t, owners)} for t in range(1, owners)] + [{"heads": lax.rem(me + u, ring)} for u in range(1, ring)])
 
     piece_rows = wo_ref.shape[0] // owners
+    spread_rows = pl.ds(0, SPREAD)
+    core = lax.rem(here, 2)
+    partner = here + 1 - 2 * core
+    chip_right, chip_left = lax.rem(here + 2, owners), lax.rem(here + owners - 2, owners)
+    across = lax.rem(here + owners // 2, owners)
+
+    def wo_columns(u, row, rows):
+        dest = lax.rem(me + u, ring)
+        return dest, wo_ref.at[pl.ds(pl.multiple_of(row, 16), rows), pl.ds(pl.multiple_of(dest * block, block), block)]
 
     def wo_bring(u):
-        dest = lax.rem(me + u, ring)
-        src = wo_ref.at[pl.ds(pl.multiple_of(here * piece_rows, piece_rows), piece_rows), pl.ds(pl.multiple_of(dest * block, block), block)]
-        return remote(src, wo_buf.at[u - 1, here], wo_send.at[u - 1], wo_recv.at[u - 1], heads=dest)
-
-    chip_right, chip_left = lax.rem(here + 2, owners), lax.rem(here + owners - 2, owners)
-    partner = here + 1 - 2 * lax.rem(here, 2)
-    across = lax.rem(here + owners // 2, owners)
-    half_rows = piece_rows // 2
+        dest, src = wo_columns(u, here * piece_rows, SPREAD)
+        return remote(src, wo_buf.at[u - 1, here, spread_rows], wo_send.at[u - 1], wo_recv.at[u - 1], heads=dest)
 
     def wo_spread(i):
-        piece = wo_buf.at[:, here]
+        piece = wo_buf.at[:, here, spread_rows]
         return remote(piece, piece, wo_send.at[3 + i], wo_recv.at[3 + i], pool=(chip_right, chip_left, partner)[i])
 
     def wo_onward(i):
-        piece = wo_buf.at[:, (chip_left, chip_right)[i], pl.ds(i * half_rows, half_rows)]
+        piece = wo_buf.at[:, (chip_left, chip_right)[i], pl.ds(i * (SPREAD // 2), SPREAD // 2)]
         return remote(piece, piece, wo_send.at[6 + i], wo_recv.at[6 + i], pool=(chip_right, chip_left)[i])
 
     def wo_beside(i):
-        piece = wo_buf.at[:, (chip_left, chip_right)[i]]
+        piece = wo_buf.at[:, (chip_left, chip_right)[i], spread_rows]
         return remote(piece, piece, wo_send.at[8 + i], wo_recv.at[8 + i], pool=partner)
 
     def wo_beside_far(i):
-        piece = wo_buf.at[:, across, pl.ds(i * half_rows, half_rows)]
+        piece = wo_buf.at[:, across, pl.ds(i * (SPREAD // 2), SPREAD // 2)]
         return remote(piece, piece, wo_send.at[10 + i], wo_recv.at[10 + i], pool=partner)
+
+    rest = piece_rows - SPREAD
+    rest_rows = pl.ds(SPREAD, rest)
+    chips = owners // 2
+
+    def wo_rest(u, i):
+        piece = 2 * i + core
+        dest, src = wo_columns(u, piece * piece_rows + SPREAD, rest)
+        return remote(src, wo_buf.at[u - 1, piece, rest_rows], rest_send.at[u - 1, i], rest_recv.at[u - 1, i], heads=dest)
+
+    def wo_hand(i):
+        piece = wo_buf.at[:, 2 * i + core, rest_rows]
+        return remote(piece, piece, rest_send.at[ring - 1, i], rest_recv.at[ring - 1, i], pool=partner)
 
     for u in range(1, ring):
         wo_bring(u).start()
+    def rest_start(i):
+        for u in (2, 1, 3):
+            wo_rest(u, i).start()
+
+    early = chips // 2
+    for i in range(early):
+        rest_start(i)
 
     def page_copy(g, t):
         dest = lax.rem(here + t, owners)
@@ -130,15 +176,15 @@
     lax.fori_loop(0, tokens // step, normalise, 0)
     kv_own.wait()
 
-    def lanes(g):
-        return pl.ds(pl.multiple_of(g * head_dim, head_dim), head_dim)
+    def all_heads(src):
+        return jnp.concatenate([gathered[src, g] for g in range(heads)], axis=-1)
 
     def a_direct(g, way):
-        piece = gathered.at[me, :, lanes(g)]
+        piece = gathered.at[me, g]
         return remote(piece, piece, a_send.at[g, 0, way], a_recv.at[g, 0, way], heads=(right, left)[way])
 
     def a_passed(g, way):
-        piece = gathered.at[(left, right)[way], pl.ds(way * half, half), lanes(g)]
+        piece = gathered.at[(left, right)[way], g, pl.ds(way * half, half)]
         return remote(piece, piece, a_send.at[g, 1, way], a_recv.at[g, 1, way], heads=(right, left)[way])
 
     def a_forward(g):
@@ -171,7 +217,7 @@
             inv_den = 1.0 / (jnp.sum(e_pre, axis=-1, keepdims=True) + jnp.sum(e_new, axis=-1, keepdims=True))
             out = jnp.dot((e_pre * inv_den).astype(BF16), vals_pre, preferred_element_type=F32)
             out = out + jnp.dot((e_new * inv_den).astype(BF16), proj[2, :seen, cols], preferred_element_type=F32)
-            gathered[me, rows, lanes(g)] = out.astype(BF16)
+            gathered[me, g, rows] = out.astype(BF16)
         for way in range(2):
             a_direct(g, way).start()
 
@@ -194,11 +240,14 @@
             attend(hp, sub)
             g = hp * per_pair + sub
 
-            @pl.when(g > 0)
+            @pl.when(g >= per_pair)
             def _():
-                a_forward(g - 1)
-
-        @pl.when(hp == pairs // 2)
+                a_forward(g - per_pair)
+
+        for i in range(early, chips):
+            pl.when(hp == i - early)(functools.partial(rest_start, i))
+
+        @pl.when(hp == 1)
         def _():
             for u in range(1, ring):
                 wo_bring(u).wait_recv()
@@ -208,9 +257,14 @@
         return carry
 
     lax.fori_loop(0, pairs, one_pair, 0)
-    a_forward(heads - 1)
     wo_own.wait()
-    total[...] = jnp.dot(gathered[me], own_wo[...], preferred_element_type=F32)
+    total[...] = jnp.dot(all_heads(me), own_wo[...], preferred_element_type=F32)
+    for g in range(heads - per_pair, heads):
+        a_forward(g)
+    for i in range(chips):
+        for u in range(1, ring):
+            wo_rest(u, i).wait_recv()
+        wo_hand(i).start()
 
     for i in range(2):
         wo_spread(i).wait_recv()
@@ -232,13 +286,15 @@
         wo_beside(i).wait_recv()
     for i in range(2):
         wo_beside_far(i).wait_recv()
+    for i in range(chips):
+        wo_hand(i).wait_recv()
 
     for n in range(2):
         cols = slice(n * block // 2, (n + 1) * block // 2)
         res = total[:, cols]
         for u in range(1, ring):
             weight = wo_buf[u - 1, :, :, cols].reshape(owners * piece_rows, block // 2)
-            res = res + jnp.dot(gathered[lax.rem(me + ring - u, ring)], weight, preferred_element_type=F32)
+            res = res + jnp.dot(all_heads(lax.rem(me + ring - u, ring)), weight, preferred_element_type=F32)
         x_cols = pl.ds(pl.multiple_of(me * block + n * (block // 2), block // 2), block // 2)
         mid_buf[:, cols] = (x_buf[:, x_cols].astype(F32) + res).astype(BF16)
     mid_copy = pltpu.make_async_copy(mid_buf, mid_ref, local_sem.at[0])
@@ -252,6 +308,10 @@
     lax.fori_loop(0, heads, page_settle, 0)
     for u in range(1, ring):
         wo_bring(u).wait_send()
+    for i in range(chips):
+        for u in range(1, ring):
+            wo_rest(u, i).wait_send()
+        wo_hand(i).wait_send()
     for i in range(3):
         wo_spread(i).wait_send()
     for i in range(2):
@@ -279,7 +339,7 @@
             pltpu.VMEM((2, 3, width, PAIR), BF16),
             pltpu.VMEM((3, tokens, PAIR), BF16),
             pltpu.VMEM(kv.shape, BF16),
-            pltpu.VMEM((ring, tokens, local), BF16),
+            pltpu.VMEM((ring, heads, tokens, head_dim), BF16),
             pltpu.VMEM((ring - 1, owners, local // owners, block), BF16),
             pltpu.VMEM((local, block), BF16),
             pltpu.VMEM((tokens, block), F32),
@@ -288,6 +348,7 @@
             dma((owners - 1, heads)), dma((owners - 1, heads)),
             dma((heads, 2, 2)), dma((heads, 2, 2)),
             dma((12,)), dma((12,)),
+            dma((ring, owners // 2)), dma((ring, owners // 2)),
         ],
         compiler_params=pltpu.CompilerParams(collective_id=call_id, has_side_effects=True, vmem_limit_bytes=VMEM_MAX),
         cost_estimate=pl.CostEstimate(flops=8 * tokens * width * local, bytes_accessed=48 * 2**20, transcendentals=heads * tokens * 3 * tokens),
@@ -570,8 +631,7 @@
         cos_tab, sin_tab = rope_tables(owners * req_pages * page_len, tokens, head_dim)
         hidden = x_tokens[0]
         for layer in range(layers):
-            picked = kv_pool.at[layer, wanted].get(mode="promise_in_bounds")
-            picked = picked.reshape(owners, req_pages, 2, page_len, kv_loc, head_dim).transpose(0, 4, 1, 2, 3, 5)
+            picked = pick_pages(kv_pool[layer], wanted, owners)
             x_mid = front(2 * layer, ring, owners, picked, hidden, w_q[layer], w_k[layer], w_v[layer], w_o[layer], gain_attn[layer][None], cos_tab, sin_tab)
             hidden = mlp(2 * layer + 1, ring, x_mid, gain_mlp[layer][None], w_gate[layer].T, w_up[layer].T, w_down[layer])
         return hidden[None]

time: 258 us -> 243 us (0.942)
  local copies, waits for them, and re-layouts: 16.5 us -> 4.7 us
  other arithmetic: 2.67 us -> 0 us
    gather x2 -> x0, local copies, waits for them, and re-layouts: 11.8 us -> none  [local_fn(): picked = kv_pool.at[layer, wanted].get(mode='promise_in_bounds')]
    pallas_call x0 -> x1, Pallas kernels: none -> 7.7 us  [pick_pages(): pl.pallas_call(pick_kernel, grid_spec=pltpu.PrefetchScalarGridSpec(num_sc...]
    pallas_call x1, Pallas kernels: 89.5 us -> 82.5 us  [front(): pl.pallas_call(functools.partial(front_kernel, ring, owners), out_shape=j...]
where the time goes in v3:
time: 243 us
  Pallas kernels  238 us (98%)
  local copies, waits for them, and re-layouts  4.7 us (2%)
    pallas_call x1, Pallas kernels, mlp(): pl.pallas_call(functools.partial(mlp_kernel, ring), out_shape=jax.ShapeDt...  148 us
    pallas_call x1, Pallas kernels, front(): pl.pallas_call(functools.partial(front_kernel, ring, owners), out_shape=j...  82.5 us
    pallas_call x1, Pallas kernels, pick_pages(): pl.pallas_call(pick_kernel, grid_spec=pltpu.PrefetchScalarGridSpec(num_sc...  7.7 us

profile of v3, /device:TPU:97, one launch (start us, length us, event | category | flops | bytes accessed | tf_op | source)
XLA Modules:
  0.0 243.1 jit_solution(15059700364887702709)
XLA Ops:
  0.0 7.7 %pick_pages.1.kv_ref = bf16[8,8,1,2,128,128]{5,4,3,2,1,0:T(8,128)(2,1)} custom-call(s32[8]{0:T(128)} %bitcast.17, bf16[16,2,128,8,128]{4,3,2,1,0:T(8,128)(2,1)} %bitcast.15), custom_call_target="tpu_custom_call" | custom-call | tf_op jit(solution)/shard_map/pick_pages/pallas_call | solution.py:34
  7.7 82.5 %front.1.x_ref = bf16[512,1024]{1,0:T(8,128)(2,1)} custom-call(bf16[8,8,1,2,128,128]{5,4,3,2,1,0:T(8,128)(2,1)} %pick_pages.1.kv_ref, bf16[512,4096]{1,0:T(8,128)(2,1)} %bitcast.25, bf16[4096,1024]{1,0:T(8,128)(2,1)} %bitcast.21, bf16[4096,1024]{1,0:T(8,128)(2,1)} %bitcast.22, bf16[4096,1024]{1,0:T(8,128)(2,1)} %bitcast.23, bf16[1024,4096]{1,0:T(8,128)(2,1)} %bitcast.24, ...), custom_call_target="tpu_custom_call" | custom-call | flops 17179869184 | bytes 50331648 | tf_op jit(solution)/shard_map/front/pallas_call | solution.py:331
  90.3 148.1 %mlp.1 = bf16[512,4096]{1,0:T(8,128)(2,1)} custom-call(bf16[512,1024]{1,0:T(8,128)(2,1)} %front.1.x_ref, bf16[1,4096]{1,0:T(2,128)(2,1)} %gain_ref.3, bf16[2752,4096]{1,0:T(8,128)(2,1)} %bitcast.18, bf16[2752,4096]{1,0:T(8,128)(2,1)} %bitcast.19, bf16[2752,4096]{1,0:T(8,128)(2,1)} %bitcast.20), custom_call_target="tpu_custom_call" | custom-call | flops 34628173824 | bytes 146800640 | tf_op jit(solution)/shard_map/mlp/pallas_call | solution.py:594
  238.4 4.7 %copy.16 = bf16[1,512,4096]{2,1,0:T(8,128)(2,1)} copy(bf16[1,512,4096]{2,1,0:T(8,128)(2,1)} %bitcast.16) | data formatting | bytes 8388608

commit v4 on v3

--- a/solution.py
+++ b/solution.py
@@ -240,9 +240,9 @@
             attend(hp, sub)
             g = hp * per_pair + sub
 
-            @pl.when(g >= per_pair)
+            @pl.when(g >= 3)
             def _():
-                a_forward(g - per_pair)
+                a_forward(g - 3)
 
         for i in range(early, chips):
             pl.when(hp == i - early)(functools.partial(rest_start, i))
@@ -259,7 +259,7 @@
     lax.fori_loop(0, pairs, one_pair, 0)
     wo_own.wait()
     total[...] = jnp.dot(all_heads(me), own_wo[...], preferred_element_type=F32)
-    for g in range(heads - per_pair, heads):
+    for g in range(heads - 3, heads):
         a_forward(g)
     for i in range(chips):
         for u in range(1, ring):
@@ -406,11 +406,6 @@
         slot = lax.rem(jj, 3)
         return pltpu.make_async_copy(wd_ref.at[:, pl.ds(col, n_half)], down_w.at[slot], d_sem.at[slot])
 
-    run(load_full(0, 0))
-    run(load_full(0, 1))
-    for jj in range(2):
-        load_down(jj).start()
-
     signal_all([{"heads": right}, {"heads": left}])
 
     def mid_direct(c, way):
@@ -548,6 +543,10 @@
 
     do = functools.partial
     mid_start(0)
+    run(load_full(0, 0))
+    run(load_full(0, 1))
+    for jj in range(2):
+        load_down(jj).start()
     mid_forward(0)
     mid_start(1)
     mid_settle(0)

time: 243 us -> 239 us (0.984)
  Pallas kernels: 238 us -> 234 us
    pallas_call x1, Pallas kernels: 148 us -> 145 us  [mlp(): pl.pallas_call(functools.partial(mlp_kernel, ring), out_shape=jax.ShapeDt...]
where the time goes in v4:
time: 239 us
  Pallas kernels  234 us (98%)
  local copies, waits for them, and re-layouts  4.7 us (2%)
    pallas_call x1, Pallas kernels, mlp(): pl.pallas_call(functools.partial(mlp_kernel, ring), out_shape=jax.ShapeDt...  145 us
    pallas_call x1, Pallas kernels, front(): pl.pallas_call(functools.partial(front_kernel, ring, owners), out_shape=j...  81 us
    pallas_call x1, Pallas kernels, pick_pages(): pl.pallas_call(pick_kernel, grid_spec=pltpu.PrefetchScalarGridSpec(num_sc...  7.7 us

profile of v4, /device:TPU:97, one launch (start us, length us, event | category | flops | bytes accessed | tf_op | source)
XLA Modules:
  0.0 238.6 jit_solution(1543323141966030287)
XLA Ops:
  0.0 7.7 %pick_pages.1.kv_ref = bf16[8,8,1,2,128,128]{5,4,3,2,1,0:T(8,128)(2,1)} custom-call(s32[8]{0:T(128)} %bitcast.17, bf16[16,2,128,8,128]{4,3,2,1,0:T(8,128)(2,1)} %bitcast.15), custom_call_target="tpu_custom_call" | custom-call | tf_op jit(solution)/shard_map/pick_pages/pallas_call | solution.py:34
  7.7 81.0 %front.1.x_ref = bf16[512,1024]{1,0:T(8,128)(2,1)} custom-call(bf16[8,8,1,2,128,128]{5,4,3,2,1,0:T(8,128)(2,1)} %pick_pages.1.kv_ref, bf16[512,4096]{1,0:T(8,128)(2,1)} %bitcast.25, bf16[4096,1024]{1,0:T(8,128)(2,1)} %bitcast.21, bf16[4096,1024]{1,0:T(8,128)(2,1)} %bitcast.22, bf16[4096,1024]{1,0:T(8,128)(2,1)} %bitcast.23, bf16[1024,4096]{1,0:T(8,128)(2,1)} %bitcast.24, ...), custom_call_target="tpu_custom_call" | custom-call | flops 17179869184 | bytes 50331648 | tf_op jit(solution)/shard_map/front/pallas_call | solution.py:331
  88.7 145.2 %mlp.1 = bf16[512,4096]{1,0:T(8,128)(2,1)} custom-call(bf16[512,1024]{1,0:T(8,128)(2,1)} %front.1.x_ref, bf16[1,4096]{1,0:T(2,128)(2,1)} %gain_ref.3, bf16[2752,4096]{1,0:T(8,128)(2,1)} %bitcast.18, bf16[2752,4096]{1,0:T(8,128)(2,1)} %bitcast.19, bf16[2752,4096]{1,0:T(8,128)(2,1)} %bitcast.20), custom_call_target="tpu_custom_call" | custom-call | flops 34628173824 | bytes 146800640 | tf_op jit(solution)/shard_map/mlp/pallas_call | solution.py:593
  233.9 4.7 %copy.16 = bf16[1,512,4096]{2,1,0:T(8,128)(2,1)} copy(bf16[1,512,4096]{2,1,0:T(8,128)(2,1)} %bitcast.16) | data formatting | bytes 8388608
